TPU v7x, 32 devices: a whole 2x2x4 slice. The times are simulated.
32 devices in a mesh: dp: 2 (over x), tp: 4 (over z), sp: 4 (over y, core).
Axes of the slice: x: 2, y: 2, z: 4, core: 2. Of those that a mesh axis runs over, the one named last changes fastest.
Arguments:
- tokens: bfloat16 [16, 3072], P(('dp', 'sp')), parts along dimension 0
- states: float32 [4, 16, 24, 128, 128], P('sp', 'dp', 'tp'), parts along dimension 1
- k_cache: bfloat16 [16, 8, 8192, 128], P('dp', 'tp', 'sp'), parts along dimension 0
- v_cache: bfloat16 [16, 8, 8192, 128], P('dp', 'tp', 'sp'), parts along dimension 0
- slopes: float32 [24], P('tp')
- lin_gain: float32 [3072], replicated
- w_lin_qkv: bfloat16 [3072, 3, 3072], P(None, None, 'tp')
- w_lin_gate: bfloat16 [3072, 3072], P(None, 'tp')
- out_gain: float32 [3072], P('tp')
- w_lin_out: bfloat16 [3072, 3072], P('tp')
- attn_gain: float32 [3072], replicated
- w_attn_in: bfloat16 [3072, 8, 5, 128], P(None, 'tp')
- w_attn_out: bfloat16 [3072, 3072], P('tp')
Outputs:
- output 1: bfloat16 [16, 3072], P(('dp', 'sp')), parts along dimension 0
- output 2: float32 [16, 24, 128, 128], P(('dp', 'sp'), 'tp'), parts along dimension 0
- output 3: bfloat16 [16, 8, 8208, 128], P(('dp', 'sp'), 'tp'), parts along dimension 0
- output 4: bfloat16 [16, 8, 8208, 128], P(('dp', 'sp'), 'tp'), parts along dimension 0
There are 2 independent parts. A program takes and returns all parts, laid end to end along the dimension named above; an argument that names none is the same for every part.
All inputs are finite; a program needn't handle non-finite values.
Results may differ from a plain program's by a relative error of at most 0.0125481.
Values are sent between devices in bfloat16 or wider.
A program may use at most 1 GiB of HBM per device.

v0:
```python
import jax
import jax.numpy as jnp
from jax import lax
from jax.sharding import PartitionSpec as P

NORM_EPS = 1e-6
ROPE_BASE = 10000000.0
RES_ALPHA = 1.0
RES_BETA = 1.0
CACHE_EXTRA = 16


def rms_norm(vals_in, gain_vec):
    vals32 = vals_in.astype(jnp.float32)
    inv_rms = lax.rsqrt(jnp.mean(vals32 * vals32, axis=-1, keepdims=True) + NORM_EPS)
    return vals32 * inv_rms * gain_vec


def rotary(vals_in, position):
    rope_dim = vals_in.shape[-1] // 2
    half_dim = rope_dim // 2
    inv_freq = ROPE_BASE ** (-jnp.arange(0, rope_dim, 2, dtype=jnp.float32) / rope_dim)
    angles = position * inv_freq
    cosine = jnp.cos(angles)
    sine_vals = jnp.sin(angles)
    vals32 = vals_in.astype(jnp.float32)
    first_half = vals32[..., :half_dim]
    second_half = vals32[..., half_dim:rope_dim]
    return jnp.concatenate([first_half * cosine - second_half * sine_vals, second_half * cosine + first_half * sine_vals, vals32[..., rope_dim:]], axis=-1).astype(jnp.bfloat16)


def lightning_layer(tokens, moved_state, slopes, lin_gain, w_lin_qkv, w_lin_gate, out_gain, w_lin_out, hidden_width):
    rows = tokens.shape[0]
    heads_dev = slopes.shape[0]
    head_dim = moved_state.shape[-1]
    normed = rms_norm(tokens, lin_gain).astype(jnp.bfloat16)
    lin_proj = jnp.einsum('bd,dkn->bkn', normed, w_lin_qkv, preferred_element_type=jnp.float32)
    act_vals = jax.nn.silu(lin_proj).astype(jnp.bfloat16).reshape(rows, 3, heads_dev, head_dim)
    state_new = jnp.exp(-slopes)[None, :, None, None] * moved_state + jnp.einsum('bhd,bhe->bhde', act_vals[:, 1], act_vals[:, 2], preferred_element_type=jnp.float32)
    lin_attn = jnp.einsum('bhd,bhde->bhe', act_vals[:, 0].astype(jnp.float32), state_new).reshape(rows, heads_dev * head_dim)
    square_sum = lax.psum(jnp.sum(lin_attn * lin_attn, axis=-1, keepdims=True), 'tp')
    inv_rms = lax.rsqrt(square_sum / hidden_width + NORM_EPS)
    gate_vals = jax.nn.sigmoid(jnp.dot(normed, w_lin_gate, preferred_element_type=jnp.float32))
    mixed_out = (lin_attn * inv_rms * out_gain * gate_vals).astype(jnp.bfloat16)
    lin_out = lax.psum(jnp.dot(mixed_out, w_lin_out, preferred_element_type=jnp.float32), 'tp')
    hidden = (RES_ALPHA * normed.astype(jnp.float32) + RES_BETA * lin_out).astype(jnp.bfloat16)
    return hidden, state_new


def solution(mesh):
    seq_shards = mesh.shape['sp']
    tp_size = mesh.shape['tp']

    def device_step(tokens, states, k_cache, v_cache, slopes, lin_gain, w_lin_qkv, w_lin_gate, out_gain, w_lin_out, attn_gain, w_attn_in, w_attn_out):
        rows = tokens.shape[0]
        kv_dev = k_cache.shape[1]
        shard_len = k_cache.shape[2]
        head_dim = k_cache.shape[3]
        group = w_attn_in.shape[2] - 2
        prompt_len = seq_shards * shard_len
        k_moved = lax.all_to_all(k_cache, 'sp', 0, 2, tiled=True)
        v_moved = lax.all_to_all(v_cache, 'sp', 0, 2, tiled=True)
        shard_idx = lax.axis_index('sp')
        offset = (shard_len * (seq_shards - 1 - shard_idx)).astype(jnp.float32)
        weighted = states[0] * jnp.exp(-slopes * offset)[None, :, None, None]
        moved_state = lax.psum_scatter(weighted, 'sp', scatter_dimension=0, tiled=True)
        hidden, state_new = lightning_layer(tokens, moved_state, slopes, lin_gain, w_lin_qkv, w_lin_gate, out_gain, w_lin_out, tp_size * slopes.shape[0] * head_dim)

        normed = rms_norm(hidden, attn_gain).astype(jnp.bfloat16)
        attn_proj = jnp.einsum('bd,dkjn->bkjn', normed, w_attn_in, preferred_element_type=jnp.float32).astype(jnp.bfloat16)
        query_rot = rotary(attn_proj[:, :, :group], prompt_len)
        key_new = rotary(attn_proj[:, :, group], prompt_len)
        value_new = attn_proj[:, :, group + 1]
        score_scale = head_dim ** -0.5
        scores = jnp.einsum('bkgd,bktd->bkgt', query_rot, k_moved, preferred_element_type=jnp.float32) * score_scale
        new_score = jnp.einsum('clhe,cle->clh', query_rot, key_new, preferred_element_type=jnp.float32) * score_scale
        row_max = jnp.maximum(jnp.max(scores, axis=-1), new_score)
        probs = jnp.exp(scores - row_max[..., None])
        new_prob = jnp.exp(new_score - row_max)
        prob_sum = jnp.sum(probs, axis=-1) + new_prob
        weighted_sum = jnp.einsum('bkgt,bktd->bkgd', probs.astype(jnp.bfloat16), v_moved, preferred_element_type=jnp.float32)
        weighted_sum = weighted_sum + new_prob.astype(jnp.bfloat16).astype(jnp.float32)[..., None] * value_new.astype(jnp.float32)[:, :, None, :]
        head_out = (weighted_sum / prob_sum[..., None]).astype(jnp.bfloat16).reshape(rows, kv_dev * group * head_dim)
        attn_out = lax.psum(jnp.dot(head_out, w_attn_out, preferred_element_type=jnp.float32), 'tp')
        hidden_out = (RES_ALPHA * normed.astype(jnp.float32) + RES_BETA * attn_out).astype(jnp.bfloat16)
        tail_zeros = jnp.zeros((rows, kv_dev, CACHE_EXTRA - 1, head_dim), jnp.bfloat16)
        k_out = jnp.concatenate([k_moved, key_new[:, :, None, :], tail_zeros], axis=2)
        v_out = jnp.concatenate([v_moved, value_new[:, :, None, :], tail_zeros], axis=2)
        return hidden_out, state_new, k_out, v_out

    batch_spec = P(('dp', 'sp'), None)
    head_spec = P(('dp', 'sp'), 'tp', None, None)
    cache_spec = P('dp', 'tp', 'sp', None)
    in_specs = (batch_spec, P('sp', 'dp', 'tp', None, None), cache_spec, cache_spec, P('tp'), P(None), P(None, None, 'tp'), P(None, 'tp'), P('tp'), P('tp', None), P(None), P(None, 'tp', None, None), P('tp', None))
    out_specs = (batch_spec, head_spec, head_spec, head_spec)
    return jax.shard_map(device_step, mesh=mesh, in_specs=in_specs, out_specs=out_specs, check_vma=False)
```

profile of v0, /device:TPU:0, one launch (start us, length us, event | category | flops | bytes accessed | tf_op | source)
XLA Modules:
  0.0 345.0 jit_solution(15161174206952135802)
XLA Ops:
  7.2 0.0 copy-start.6
  7.2 0.0 copy-start
  7.2 5.9 %all-to-all-start.1 = ((bf16[8,2,2048,128]{3,2,1,0:T(8,128)(2,1)}), bf16[8,2,2048,128]{3,2,1,0:T(8,128)(2,1)}, u32[]{:S(2)}, u32[]{:S(2)}) async-start(bf16[8,2,2048,128]{3,2,1,0:T(8,128)(2,1)} %param.16), calls=%async_computation.2 | async-start | bytes 16777216 | tf_op jit(solution)/shard_map/all_to_all | solution.py:62
  13.1 0.0 reduce-scatter.2.cloned.1.call-start
  13.2 0.0 copy-done.6
  13.2 0.0 copy-done
  13.2 2.1 bitcast_multiply_fusion
  15.3 0.0 reduce-scatter.2.cloned.1.call-update
  15.3 0.0 copy-start.2
  15.3 0.0 copy-start.3
  15.3 108.2 %all-to-all-done.1 = bf16[8,2,2048,128]{3,2,1,0:T(8,128)(2,1)} async-done(((bf16[8,2,2048,128]{3,2,1,0:T(8,128)(2,1)}), bf16[8,2,2048,128]{3,2,1,0:T(8,128)(2,1)}, u32[]{:S(2)}, u32[]{:S(2)}) %all-to-all-start.1) | async-done | bytes 8388640 | tf_op jit(solution)/shard_map/all_to_all | solution.py:62
  123.5 5.7 %all-to-all-start = ((bf16[8,2,2048,128]{3,2,1,0:T(8,128)(2,1)}), bf16[8,2,2048,128]{3,2,1,0:T(8,128)(2,1)}, u32[]{:S(2)}, u32[]{:S(2)}) async-start(bf16[8,2,2048,128]{3,2,1,0:T(8,128)(2,1)} %param.15), calls=%async_computation.1 | async-start | bytes 16777216 | tf_op jit(solution)/shard_map/all_to_all | solution.py:61
  129.2 0.0 copy-done.2
  129.2 0.1 fusion.17
  129.4 7.0 %fusion.23 = bf16[2,3,768]{2,0,1:T(2,128)(2,1)S(1)} fusion(bf16[3072,3,768]{2,0,1:T(8,128)(2,1)} %param.19, bf16[2,3072]{1,0:T(2,128)(2,1)S(1)} %copy-done.2, f32[2]{0:T(128)S(1)} %add_rsqrt_fusion.1, f32[3072]{0:T(1024)S(1)} %copy-done.3), kind=kOutput, calls=%fused_computation.33 | convolution fusion | flops 28359168 | bytes 14189576 | tf_op jit(solution)/shard_map/bd,dkn->bkn/dot_general | solution.py:37
  136.4 0.1 fusion.43
  136.5 0.0 reduce-scatter.2.cloned.1.call-done
  136.5 1.4 multiply_add_fusion
  137.9 0.0 copy-start.1
  138.0 0.2 fusion.31
  138.2 0.1 fusion.27
  138.3 12.7 %psum.21 = f32[2,1]{0,1:T(1,128)S(1)} all-reduce(f32[2,1]{0,1:T(1,128)S(1)} %bitcast.86), channel_id=1, replica_groups=mesh['dp'=2,'tp'=4,'sp'=4] {'tp'}, use_global_device_ids=true, to_apply=%region_3.4 | all-reduce | flops 2 | bytes 16 | tf_op jit(solution)/shard_map/psum | solution.py:41
  151.0 7.4 %copy.31 = bf16[4,2,2,2048,128]{4,3,0,2,1:T(8,128)(2,1)} copy(bf16[4,2,2,2048,128]{4,3,2,1,0:T(8,128)(2,1)} %bitcast.19) | data formatting | bytes 16777216 | tf_op jit(solution)/shard_map/all_to_all | solution.py:62
  158.4 0.0 copy-done.1
  158.4 5.6 %fusion.12 = f32[2,3072]{1,0:T(2,128)S(1)} fusion(bf16[768,3072]{1,0:T(8,128)(2,1)} %param.22, bf16[3072,768]{1,0:T(8,128)(2,1)} %param.20, f32[1,2,6,128]{3,2,1,0:T(8,128)S(1)} %bitcast.81, f32[2]{0:T(128)S(1)} %rsqrt_bitcast_fusion, f32[768]{0:T(1024)S(1)} %copy-done.5, bf16[2,3072]{1,0:T(2,128)(2,1)S(1)} %copy-done.2, f32[2]{0:T(128)S(1)} %add_rsqrt_fusion.1, ...), kind=kOutput, calls=%fused_computation.14 | convolution fusion | flops 18909696 | bytes 9495568 | tf_op jit(solution)/shard_map/dot_general | solution.py:45
  164.0 15.8 %psum.22 = f32[2,3072]{1,0:T(2,128)S(1)} all-reduce(f32[2,3072]{1,0:T(2,128)S(1)} %fusion.12), channel_id=1, replica_groups=mesh['dp'=2,'tp'=4,'sp'=4] {'tp'}, use_global_device_ids=true, to_apply=%region_4.5 | all-reduce | flops 6144 | bytes 49152 | tf_op jit(solution)/shard_map/psum | solution.py:45
  179.8 0.2 fusion.20
  180.0 0.1 fusion.22
  180.1 4.4 %fusion.3 = bf16[2,2,5,128]{3,0,2,1:T(2,128)(2,1)S(1)} fusion(bf16[3072,2,5,128]{3,1,2,0:T(2,128)(2,1)} %param.24, bf16[2,3072]{1,0:T(2,128)(2,1)S(1)} %fusion.22), kind=kOutput, calls=%fused_computation.6 | convolution fusion | flops 15731200 | bytes 7881728 | tf_op jit(solution)/shard_map/bd,dkjn->bkjn/dot_general | solution.py:70
  184.5 0.1 slice.56
  184.6 0.1 slice.83
  184.7 0.1 slice_bitcast_fusion.4
  184.7 37.3 %all-to-all-done = bf16[8,2,2048,128]{3,2,1,0:T(8,128)(2,1)} async-done(((bf16[8,2,2048,128]{3,2,1,0:T(8,128)(2,1)}), bf16[8,2,2048,128]{3,2,1,0:T(8,128)(2,1)}, u32[]{:S(2)}, u32[]{:S(2)}) %all-to-all-start) | async-done | bytes 8388640 | tf_op jit(solution)/shard_map/all_to_all | solution.py:61
  222.0 7.6 %copy.29 = bf16[4,2,2,2048,128]{4,3,0,2,1:T(8,128)(2,1)} copy(bf16[4,2,2,2048,128]{4,3,2,1,0:T(8,128)(2,1)} %bitcast.11) | data formatting | bytes 16777216 | tf_op jit(solution)/shard_map/all_to_all | solution.py:61
  229.6 0.1 subtract_convert_fusion.1
  229.7 0.1 subtract_convert_fusion
  229.8 0.1 pad_maximum_fusion
  229.9 5.7 %fusion.48 = (f32[2,2,3]{2,1,0:T(2,128)S(1)}, f32[2,2,3,8192]{3,2,1,0:T(4,128)S(1)}) fusion(bf16[2,2,8192,128]{3,2,1,0:T(8,128)(2,1)} %bitcast.79, bf16[2,2,3,128]{3,0,2,1:T(2,128)(2,1)S(1)} %pad_maximum_fusion), kind=kOutput, calls=%fused_computation.83 | convolution fusion | flops 25362420 | bytes 8784944 | tf_op jit(solution)/shard_map/bkgd,bktd->bkgt/dot_general | solution.py:75
  235.6 0.1 maximum_bitcast_fusion
  235.7 0.1 fusion.35
  235.8 0.4 fusion.13
  236.2 4.7 %fusion.6 = bf16[2,2,3,128]{3,2,1,0:T(4,128)(2,1)S(1)} fusion(bf16[2,2,8192,128]{3,2,1,0:T(8,128)(2,1)} %bitcast.77, f32[2,2,3,8192]{3,2,1,0:T(4,128)S(1)} %get-tuple-element.19, f32[2,2,3]{2,1,0:T(2,128)S(1)} %multiply_maximum_fusion, f32[2,2,3]{2,1,0:T(2,128)S(1)} %get-tuple-element.13, f32[2,2,128]{2,1,0:T(2,128)S(1)} %copy.32, ...), kind=kOutput, calls=%fused_computation.7 | convolution fusion | flops 25368576 | bytes 8787088 | tf_op jit(solution)/shard_map/bkgt,bktd->bkgd/dot_general | solution.py:81
  240.9 3.1 fusion.49
  244.0 20.0 %psum.23 = f32[2,3072]{1,0:T(2,128)S(1)} all-reduce(f32[2,3072]{1,0:T(2,128)S(1)} %fusion.49), channel_id=1, replica_groups=mesh['dp'=2,'tp'=4,'sp'=4] {'tp'}, use_global_device_ids=true, to_apply=%region_8.9 | all-reduce | flops 6144 | bytes 49152 | tf_op jit(solution)/shard_map/psum | solution.py:84
  264.0 0.6 add_convert_fusion
  264.6 0.1 pad_maximum_fusion.1
  264.7 36.7 %concatenate.36 = bf16[2,2,8208,128]{3,2,1,0:T(8,128)(2,1)} concatenate(bf16[2,2,8192,128]{3,2,1,0:T(8,128)(2,1)} %bitcast.80, bf16[2,2,1,128]{3,2,1,0:T(2,128)(2,1)S(1)} %copy.37, bf16[2,2,15,128]{3,2,1,0:T(8,128)(2,1)S(1)} %broadcast_in_dim.5), dimensions={2} | concatenate | bytes 16809984 | tf_op jit(solution)/shard_map/concatenate | solution.py:87
  301.4 36.7 %concatenate.37 = bf16[2,2,8208,128]{3,2,1,0:T(8,128)(2,1)} concatenate(bf16[2,2,8192,128]{3,2,1,0:T(8,128)(2,1)} %bitcast.78, bf16[2,2,1,128]{3,2,1,0:T(2,128)(2,1)S(1)} %copy.38, bf16[2,2,15,128]{3,2,1,0:T(8,128)(2,1)S(1)} %broadcast_in_dim.5), dimensions={2} | concatenate | bytes 16809984 | tf_op jit(solution)/shard_map/concatenate | solution.py:88
  (21 shorter events, 0.1 us)
Async XLA Ops:
  7.2 6.0 %copy-start.6 = (f32[6]{0:T(128)S(1)}, f32[6]{0:T(128)}, u32[]{:S(2)}) copy-start(f32[6]{0:T(128)} %param.17) | copy-start | bytes 76
  7.2 6.0 %copy-start = (f32[1,8,6,128,128]{4,3,2,1,0:T(8,128)S(1)}, f32[1,8,6,128,128]{4,3,2,1,0:T(8,128)}, u32[]{:S(2)}) copy-start(f32[1,8,6,128,128]{4,3,2,1,0:T(8,128)} %param.14) | copy-start | bytes 9437188
  7.2 116.3 %all-to-all-start.1 = ((bf16[8,2,2048,128]{3,2,1,0:T(8,128)(2,1)}), bf16[8,2,2048,128]{3,2,1,0:T(8,128)(2,1)}, u32[]{:S(2)}, u32[]{:S(2)}) async-start(bf16[8,2,2048,128]{3,2,1,0:T(8,128)(2,1)} %param.16), calls=%async_computation.2 | async-start | bytes 16777216 | tf_op jit(solution)/shard_map/all_to_all | solution.py:62
  13.1 123.4 %reduce-scatter.2.cloned.1.call-start = ((), (), s32[]{:S(2)}) async-start(), calls=%async_computation.3 | async-start | bytes 3932160 | tf_op jit(solution)/shard_map/reduce_scatter | solution.py:66
  15.3 113.9 %copy-start.2 = (bf16[2,3072]{1,0:T(2,128)(2,1)S(1)}, bf16[2,3072]{1,0:T(2,128)(2,1)}, u32[]{:S(2)}) copy-start(bf16[2,3072]{1,0:T(2,128)(2,1)} %param.13) | copy-start | bytes 36868
  15.3 114.1 %copy-start.3 = (f32[3072]{0:T(1024)S(1)}, f32[3072]{0:T(1024)}, u32[]{:S(2)}) copy-start(f32[3072]{0:T(1024)} %param.18) | copy-start | bytes 36868
  123.5 98.5 %all-to-all-start = ((bf16[8,2,2048,128]{3,2,1,0:T(8,128)(2,1)}), bf16[8,2,2048,128]{3,2,1,0:T(8,128)(2,1)}, u32[]{:S(2)}, u32[]{:S(2)}) async-start(bf16[8,2,2048,128]{3,2,1,0:T(8,128)(2,1)} %param.15), calls=%async_computation.1 | async-start | bytes 16777216 | tf_op jit(solution)/shard_map/all_to_all | solution.py:61
  137.9 20.5 %copy-start.1 = (f32[2,6,128,128]{3,2,1,0:T(8,128)}, f32[2,6,128,128]{3,2,1,0:T(8,128)S(1)}, u32[]{:S(2)}) copy-start(f32[2,6,128,128]{3,2,1,0:T(8,128)S(1)} %multiply_add_fusion) | copy-start | bytes 2359300
  151.0 7.4 %copy-start.5 = (f32[768]{0:T(1024)S(1)}, f32[768]{0:T(1024)}, u32[]{:S(2)}) copy-start(f32[768]{0:T(1024)} %param.21) | copy-start | bytes 9220
  158.4 21.6 %copy-start.4 = (f32[3072]{0:T(1024)S(1)}, f32[3072]{0:T(1024)}, u32[]{:S(2)}) copy-start(f32[3072]{0:T(1024)} %param.23) | copy-start | bytes 36868
Sparse Core Ops, SparseCore 0:
  17.0 57.8 reduce-scatter.1
where the time goes:
time: 347 us; the launch traced here: 345 us
  waiting for transfers between devices  146 us (42%)
  local copies, waits for them, and re-layouts  88.8 us (26%)
  blocking collectives  48.5 us (14%)
  matrix products  30.7 us (9%)
  between operations  14.2 us (4%)
  starting transfers between devices  11.7 us (3%)
  other arithmetic  5.52 us (2%)
    all_to_all x1, waiting for transfers between devices, device_step(): v_moved = lax.all_to_all(v_cache, 'sp', 0, 2, tiled=True)  108 us
    all_to_all x1, waiting for transfers between devices, device_step(): k_moved = lax.all_to_all(k_cache, 'sp', 0, 2, tiled=True)  37.3 us
    concatenate x1, local copies, waits for them, and re-layouts, device_step(): jnp.concatenate([v_moved, value_new[:, :, None, :], tail_zeros], axis=2)  36.7 us
    concatenate x1, local copies, waits for them, and re-layouts, device_step(): jnp.concatenate([k_moved, key_new[:, :, None, :], tail_zeros], axis=2)  36.7 us
    psum x1, blocking collectives, device_step(): lax.psum(jnp.dot(head_out, w_attn_out, preferred_element_type=jnp.float32...  20 us
    psum x1, blocking collectives, lightning_layer(): lax.psum(jnp.dot(mixed_out, w_lin_out, preferred_element_type=jnp.float32...  15.8 us
    psum x1, blocking collectives, lightning_layer(): lax.psum(jnp.sum(lin_attn * lin_attn, axis=-1, keepdims=True), 'tp')  12.7 us
    all_to_all x1, local copies, waits for them, and re-layouts, device_step(): k_moved = lax.all_to_all(k_cache, 'sp', 0, 2, tiled=True)  7.59 us
  transfers between devices with their start and end apart: 3, of which 2 were waited for; matrix products, arithmetic and copies ran while one was open for 8% of the time, Pallas kernels for 0%

commit v1 on v0

v1 whole, which is shorter than its diff:
```python
import math

import jax
import jax.numpy as jnp
import numpy as np
from jax import lax
from jax.experimental import pallas as pl
from jax.experimental.pallas import tpu as pltpu
from jax.sharding import PartitionSpec as P

NORM_EPS = 1e-6
ROPE_BASE = 10000000.0
RES_ALPHA = 1.0
RES_BETA = 1.0
CACHE_EXTRA = 16

MESH = pl.DeviceIdType.MESH
F32 = jnp.float32
BF16 = jnp.bfloat16
MIB = 2**20

ST_OWN, ST_FWD, ST_SUM = 0, 1, 2
SQ, PO, PA = 3, 6, 9
QX, MX, OX = 12, 15, 18
KV_NEAR = 21
KV_FAR = 23
NUM_SEMS = KV_FAR + 16


def rope_table(head_dim, position):
    rope_dim = head_dim // 2
    half = rope_dim // 2
    inv_freq = ROPE_BASE ** (-np.arange(0, rope_dim, 2, dtype=np.float64) / rope_dim)
    cos, sin = np.cos(position * inv_freq), np.sin(position * inv_freq)
    table = np.zeros((8, head_dim), np.float32)
    table[0] = np.concatenate([cos, cos, np.ones(head_dim - rope_dim)])
    table[1, :rope_dim] = np.concatenate([-sin, sin])
    return table


def flip(index, mask):
    chip, core = index // 2, index % 2
    if mask & 2:
        chip = 1 - chip
    if mask & 1:
        core = 1 - core
    return chip * 2 + core


def silu(x):
    return x * (1.0 / (1.0 + jnp.exp(-x)))


def step_kernel(
    tokens, states, k_cache, v_cache, slopes, lin_gain, w_qkv, w_gate, out_gain, w_lin_out, attn_gain, w_in, w_attn_out, rope,
    k_buf, v_buf, s_out, hid,
    tok_v, lg_v, og_v, ag_v, rope_v, slope_s, qkv_v, gate_v, lout_v, in_v, aout_v,
    st_loc, st_rcv, st_sum, st_in, hb, rows_v, o_v, g_v, rep_v, acc_v, proj_v, qf_v, vf_v, q_all, sc_v, mrow_v, m_all, mcol_v,
    ns_v, ol_v, olr_v, ho_v, sq_all, po_all, pa_all, kst,
    send, recv, lsem, ksem,
):
    sp = lax.axis_index("sp")
    tp = lax.axis_index("tp")
    shard_len = k_cache.shape[2]
    kv_dev = k_cache.shape[1]
    head_dim = k_cache.shape[3]
    heads = slopes.shape[0]
    rows = tokens.shape[0]
    width = tokens.shape[1]
    group = heads // kv_dev
    prompt = 4 * shard_len
    local_w = heads * head_dim

    def to_sp(mask):
        return {"sp": flip(sp, mask)}

    def to_tp(off):
        return {"tp": lax.rem(tp + off, 4)}

    barrier = pltpu.get_barrier_semaphore()
    for i in (1, 2, 3):
        pl.semaphore_signal(barrier, inc=1, device_id=to_sp(i), device_id_type=MESH)
    for i in (1, 2, 3):
        pl.semaphore_signal(barrier, inc=1, device_id=to_tp(i), device_id_type=MESH)
    pl.semaphore_wait(barrier, 6)

    def remote(src, dst, i, dev):
        return pltpu.make_async_remote_copy(src, dst, send.at[i], recv.at[i], device_id=dev, device_id_type=MESH)

    def local(src, dst, i):
        return pltpu.make_async_copy(src, dst, lsem.at[i])

    my_rows = pl.ds(pl.multiple_of(sp * shard_len, shard_len), shard_len)
    far = []
    for t, (src, dst) in enumerate(((k_cache, k_buf), (v_cache, v_buf))):
        for b in range(rows):
            for j in range(kv_dev):
                for mask in (2, 3):
                    far.append(remote(src.at[flip(sp, mask) * rows + b, j], dst.at[b, j, my_rows], KV_FAR + len(far), to_sp(mask)))
    far_state = [0, 0]

    def start_far(n):
        for _ in range(n):
            if far_state[0] < len(far):
                far[far_state[0]].start()
                far_state[0] += 1

    def pump(n):
        for _ in range(n):
            far[far_state[1]].wait_send()
            far_state[1] += 1
            start_far(1)

    def st_rows(g):
        return pl.ds(g * rows, rows)

    st_own = remote(states.at[0, st_rows(flip(sp, 1))], st_rcv.at[0], ST_OWN, to_sp(1))
    st_fwd = remote(states.at[0, st_rows(flip(sp, 3))], st_rcv.at[1], ST_FWD, to_sp(1))
    st_fwd.start()
    start_far(1)
    ld_fwd = local(states.at[0, st_rows(flip(sp, 2))], st_loc.at[1], 0)
    ld_slope = local(slopes, slope_s, 1)
    ld_fwd.start()
    ld_slope.start()
    st_own.start()
    ld_own = local(states.at[0, st_rows(sp)], st_loc.at[0], 2)
    ld_tok = local(tokens, tok_v, 3)
    ld_lg = local(lin_gain, lg_v, 4)
    ld_og = local(out_gain, og_v, 5)
    ld_ag = local(attn_gain, ag_v, 6)
    ld_rope = local(rope, rope_v, 7)
    ld_qkv = [local(w_qkv.at[j], qkv_v.at[j], 8 + j) for j in range(3)]
    ld_gate = local(w_gate, gate_v, 11)
    ld_lout = local(w_lin_out, lout_v, 12)
    ld_in = local(w_in, in_v, 13)
    ld_aout = local(w_attn_out, aout_v, 14)
    own_kv = [local(src.at[st_rows(sp)], dst.at[:, :, my_rows], 15 + t) for t, (src, dst) in enumerate(((k_cache, k_buf), (v_cache, v_buf)))]
    near = [remote(src.at[st_rows(flip(sp, 1))], dst.at[:, :, my_rows], KV_NEAR + t, to_sp(1)) for t, (src, dst) in enumerate(((k_cache, k_buf), (v_cache, v_buf)))]
    for c in [ld_own, ld_tok, ld_lg, ld_og, ld_ag, ld_rope] + ld_qkv + [ld_gate, ld_lout, ld_in, ld_aout] + near + own_kv:
        c.start()

    def decay(h, shard):
        off = (shard_len * (3 - shard)).astype(F32)
        return jnp.exp(jnp.full((1, head_dim), -slope_s[h] * off, F32))

    ld_slope.wait()
    ld_fwd.wait()
    st_fwd.wait_recv()
    for h in range(heads):
        w_me, w_ot = decay(h, sp), decay(h, flip(sp, 1))
        for b in range(rows):
            st_sum[b, h] = w_me * st_loc[1, b, h] + w_ot * st_rcv[1, b, h]
    st_send = remote(st_sum, st_in, ST_SUM, to_sp(2))
    st_send.start()
    start_far(2)

    ld_tok.wait()
    ld_lg.wait()
    x = tok_v[...].astype(F32)
    inv = lax.rsqrt(jnp.mean(x * x, axis=-1, keepdims=True) + NORM_EPS)
    hb[...] = (x * inv * lg_v[...]).astype(BF16)

    def matvec(x_ref, w_ref, k_len, n_len, kb, out_dtype=F32):
        def body(k, acc):
            at = pl.ds(pl.multiple_of(k * kb, kb), kb)
            return acc + jnp.dot(x_ref[:, at], w_ref[at, :], preferred_element_type=F32)
        return lax.fori_loop(0, k_len // kb, body, jnp.zeros((rows, n_len), F32))

    acts = []
    for j in range(3):
        ld_qkv[j].wait()
        acts.append(silu(matvec(hb, qkv_v.at[j], width, local_w, 256)).astype(BF16).astype(F32))
    ld_gate.wait()
    gate = 1.0 / (1.0 + jnp.exp(-matvec(hb, gate_v, width, local_w, 256)))
    rows_v[...] = jnp.zeros_like(rows_v)
    for b in range(rows):
        for h in range(heads):
            cols = slice(h * head_dim, (h + 1) * head_dim)
            rows_v[pl.ds(b * 8 + h, 1), :] = acts[0][b:b + 1, cols]
            rows_v[pl.ds(16 + b * 8 + h, 1), :] = acts[1][b:b + 1, cols]
    cols_t = jnp.transpose(rows_v[...])

    ld_own.wait()
    st_own.wait_recv()
    st_send.wait_recv()
    for h in range(heads):
        w_me, w_ot = decay(h, sp), decay(h, flip(sp, 1))
        lam = jnp.exp(jnp.full((1, head_dim), -slope_s[h], F32))
        cols = slice(h * head_dim, (h + 1) * head_dim)
        for b in range(rows):
            moved = w_me * st_loc[0, b, h] + w_ot * st_rcv[0, b, h] + st_in[b, h]
            q_col = cols_t[:, b * 8 + h:b * 8 + h + 1]
            k_col = cols_t[:, 16 + b * 8 + h:16 + b * 8 + h + 1]
            new = lam * moved + k_col * acts[2][b:b + 1, cols]
            s_out[b, h] = new
            o_v[pl.ds(b, 1), cols] = jnp.sum(q_col * new, axis=0, keepdims=True)
    o = o_v[...]

    def gather_tp(ref, base):
        cs = [remote(ref.at[tp], ref.at[tp], base + i - 1, to_tp(i)) for i in (1, 2, 3)]
        for c in cs:
            c.start()
        return cs

    def settle(cs):
        for c in cs:
            c.wait_recv()
        for c in cs:
            c.wait_send()

    sq_all[tp] = jnp.broadcast_to(jnp.sum(o * o, axis=-1, keepdims=True), (rows, 128))
    cs = gather_tp(sq_all, SQ)
    pump(1)
    ld_og.wait()
    settle(cs)
    sq = ((sq_all[0] + sq_all[1]) + sq_all[2]) + sq_all[3]
    inv = lax.rsqrt(sq[:, :1] / (4 * local_w) + NORM_EPS)
    g_v[...] = (o * inv * og_v[...] * gate).astype(BF16)

    def project(x_ref, w_ref, dst):
        nb = 512

        def body(n, _):
            at = pl.ds(pl.multiple_of(n * nb, nb), nb)
            dst[tp, :, at] = jnp.dot(x_ref[...], w_ref[:, at], preferred_element_type=F32)
            return 0
        lax.fori_loop(0, width // nb, body, 0)

    ld_lout.wait()
    project(g_v, lout_v, po_all)
    cs = gather_tp(po_all, PO)
    reps = in_v.shape[0] // width
    d_id = lax.broadcasted_iota(jnp.int32, rep_v.shape, 0)
    l_id = lax.broadcasted_iota(jnp.int32, rep_v.shape, 1)
    rep_v[...] = jnp.where((l_id >= d_id * reps) & (l_id < d_id * reps + reps), 1.0, 0.0).astype(BF16)
    settle(cs)
    lin = ((po_all[0] + po_all[1]) + po_all[2]) + po_all[3]
    y = (RES_ALPHA * hb[...].astype(F32) + RES_BETA * lin).astype(BF16).astype(F32)

    ld_ag.wait()
    inv = lax.rsqrt(jnp.mean(y * y, axis=-1, keepdims=True) + NORM_EPS)
    hb[...] = (y * inv * ag_v[...]).astype(BF16)
    ld_in.wait()
    ld_rope.wait()
    lane = lax.broadcasted_iota(jnp.int32, (16, 128 * reps), 1)
    sub = lax.broadcasted_iota(jnp.int32, (16, 128 * reps), 0)
    pick = lax.rem(lane, reps) == sub

    def in_body(d, acc):
        xb = hb[:, pl.ds(pl.multiple_of(d * 128, 128), 128)]
        xr = jnp.dot(xb, rep_v[...], preferred_element_type=F32)
        lhs = jnp.concatenate([jnp.where(pick, xr[b:b + 1], 0.0) for b in range(rows)], axis=0).astype(BF16)
        w = in_v[pl.ds(pl.multiple_of(d * 128 * reps, 128), 128 * reps), :]
        return acc + jnp.dot(lhs, w, preferred_element_type=F32)

    proj = lax.fori_loop(0, width // 128, in_body, jnp.zeros((16 * rows, head_dim), F32)).astype(BF16).astype(F32)
    lane = lax.broadcasted_iota(jnp.int32, proj.shape, 1)
    quarter = head_dim // 4
    partner = jnp.where(lane < quarter, pltpu.roll(proj, head_dim - quarter, 1), pltpu.roll(proj, quarter, 1))
    proj_v[...] = proj
    acc_v[...] = (proj * rope_v[0:1] + partner * rope_v[1:2]).astype(BF16).astype(F32)
    qf_v[...] = jnp.zeros_like(qf_v)
    ns_v[...] = jnp.zeros_like(ns_v)
    tail_row = lax.broadcasted_iota(jnp.int32, (CACHE_EXTRA, head_dim), 0)
    for b in range(rows):
        for j in range(kv_dev):
            p = b * kv_dev + j
            for g in range(group):
                qf_v[pl.ds(p * 8 + g, 1), :] = acc_v[pl.ds(b * 16 + g * kv_dev + j, 1), :]
            k_new = acc_v[pl.ds(b * 16 + group * kv_dev + j, 1), :]
            v_new = proj_v[pl.ds(b * 16 + (group + 1) * kv_dev + j, 1), :]
            k_buf[b, j, pl.ds(prompt, CACHE_EXTRA), :] = jnp.where(tail_row == 0, k_new, 0.0).astype(BF16)
            v_buf[b, j, pl.ds(prompt, CACHE_EXTRA), :] = jnp.where(tail_row == 0, v_new, 0.0).astype(BF16)
            vf_v[pl.ds(p * 8, 8), :] = jnp.broadcast_to(v_new, (8, head_dim))
            ns_v[pl.ds(p * 8, 8), :] = jnp.broadcast_to(k_new, (8, head_dim))
    qf = qf_v[...]
    pairs = rows * kv_dev
    my_pairs = pl.ds(sp * pairs, pairs)
    q_all[my_pairs] = qf.astype(BF16).reshape(pairs, 8, head_dim)
    cs = [remote(q_all.at[my_pairs], q_all.at[my_pairs], QX + i - 1, to_sp(i)) for i in (1, 2, 3)]
    for c in cs:
        c.start()
    pump(2)
    scale = head_dim ** -0.5
    ns_v[...] = jnp.broadcast_to(jnp.sum(qf * ns_v[...], axis=-1, keepdims=True) * scale, ns_v.shape)

    n_pairs = 4 * pairs
    slots = kst.shape[0]

    def fetch(cache, i):
        slot = lax.rem(i, slots)
        return pltpu.make_async_copy(cache.at[i // kv_dev, lax.rem(i, kv_dev)], kst.at[slot], ksem.at[slot])

    def stream(cache, first, body):
        def step(i, _):
            fetch(cache, i).wait()
            body(i, kst[lax.rem(i, slots)])

            @pl.when(i + slots < n_pairs)
            def _():
                fetch(cache, i + slots).start()
            return 0
        lax.fori_loop(0, n_pairs, step, 0)

    for i in range(slots):
        fetch(k_cache, jnp.int32(i)).start()
    settle(cs)
    pump(1)

    def score_body(i, keys):
        s = lax.dot_general(q_all[i], keys, (((1,), (1,)), ((), ())), preferred_element_type=F32) * scale
        sc_v[i] = s
        mrow_v[pl.ds(pl.multiple_of(i * 8, 8), 8), :] = jnp.broadcast_to(jnp.max(s, axis=-1, keepdims=True), (8, 128))

    stream(k_cache, 0, score_body)
    for i in range(slots):
        fetch(v_cache, jnp.int32(i)).start()
    my_m = pl.ds(pl.multiple_of(sp * pairs * 8, 8), pairs * 8)
    mrow_v[my_m, :] = jnp.maximum(mrow_v[my_m, :], ns_v[...])
    m_all[sp] = jnp.transpose(mrow_v[...])[:8]
    cs = [remote(m_all.at[sp], m_all.at[sp], MX + i - 1, to_sp(i)) for i in (1, 2, 3)]
    for c in cs:
        c.start()
    pump(1)
    settle(cs)
    m = jnp.maximum(jnp.maximum(m_all[0], m_all[1]), jnp.maximum(m_all[2], m_all[3]))
    mcol_v[...] = jnp.transpose(jnp.broadcast_to(m[:1], (128, 128)))
    pump(1)
    sub = lax.broadcasted_iota(jnp.int32, (8, head_dim), 0)

    def out_body(i, values):
        p = jnp.exp(sc_v[i] - mcol_v[pl.ds(pl.multiple_of(i * 8, 8), 8), :][:, :1])
        total = jnp.broadcast_to(jnp.sum(p, axis=-1, keepdims=True), (8, head_dim))
        o = jnp.dot(p.astype(BF16), values, preferred_element_type=F32)
        ol_v[i] = jnp.where(sub < group, o, pltpu.roll(total, group, 0))

    stream(v_cache, 0, out_body)
    cs = [remote(ol_v.at[pl.ds(flip(sp, i) * pairs, pairs)], olr_v.at[sp], OX + i - 1, to_sp(i)) for i in (1, 2, 3)]
    for c in cs:
        c.start()
    olr_v[sp] = ol_v[my_pairs]
    pump(1)
    settle(cs)
    total = (((olr_v[0] + olr_v[1]) + olr_v[2]) + olr_v[3]).reshape(pairs * 8, head_dim)
    new_p = jnp.exp(ns_v[...] - mcol_v[my_m, :])
    denom = pltpu.roll(total, pairs * 8 - group, 0) + new_p
    numer = total + new_p.astype(BF16).astype(F32) * vf_v[...]
    qf_v[...] = numer / denom
    for b in range(rows):
        for j in range(kv_dev):
            for g in range(group):
                h = j * group + g
                ho_v[pl.ds(b, 1), h * head_dim:(h + 1) * head_dim] = qf_v[pl.ds((b * kv_dev + j) * 8 + g, 1), :]
    g_v[...] = ho_v[...].astype(BF16)
    ld_aout.wait()
    project(g_v, aout_v, pa_all)
    cs = gather_tp(pa_all, PA)
    start_far(len(far))
    settle(cs)
    att = ((pa_all[0] + pa_all[1]) + pa_all[2]) + pa_all[3]
    hid[...] = (RES_ALPHA * hb[...].astype(F32) + RES_BETA * att).astype(BF16)

    st_own.wait_send()
    st_fwd.wait_send()
    st_send.wait_send()
    for c in own_kv:
        c.wait()
    for c in near:
        c.wait()
    for c in far[far_state[1]:]:
        c.wait_send()
    for c in far:
        c.wait_recv()


def write_kernel(k_buf, v_buf, s_buf, hid_buf, hid, s_out, k_out, v_out, sem):
    cs = []
    for src, dst in ((k_buf, k_out), (v_buf, v_out)):
        for b in range(src.shape[0]):
            for j in range(src.shape[1]):
                cs.append(pltpu.make_async_copy(src.at[b, j], dst.at[b, j], sem.at[len(cs)]))
    cs.append(pltpu.make_async_copy(s_buf, s_out, sem.at[len(cs)]))
    cs.append(pltpu.make_async_copy(hid_buf, hid, sem.at[len(cs)]))
    for c in cs:
        c.start()
    for c in cs:
        c.wait()


def solution(mesh):
    def device_step(tokens, states, k_cache, v_cache, slopes, lin_gain, w_lin_qkv, w_lin_gate, out_gain, w_lin_out, attn_gain, w_attn_in, w_attn_out):
        rows, width = tokens.shape
        seqs, kv_dev, shard_len, head_dim = k_cache.shape
        heads = slopes.shape[0]
        local_w = heads * head_dim
        prompt = 4 * shard_len
        reps = w_attn_in.shape[1] * w_attn_in.shape[2]
        pairs = rows * kv_dev
        cache_shape = (rows, kv_dev, prompt + CACHE_EXTRA, head_dim)
        state_shape = (rows, heads, head_dim, head_dim)
        vm, any_ = pltpu.VMEM, pl.ANY
        w_qkv = jnp.transpose(w_lin_qkv, (1, 0, 2))
        w_in = jnp.transpose(w_attn_in, (0, 2, 1, 3)).reshape(width * reps, head_dim)
        rope = jnp.asarray(rope_table(head_dim, prompt))
        dma = pltpu.SemaphoreType.DMA
        k_buf, v_buf, s_buf, hid_buf = pl.pallas_call(
            step_kernel,
            name="step",
            out_shape=(vm(cache_shape, BF16), vm(cache_shape, BF16), vm(state_shape, F32), vm((rows, width), BF16)),
            in_specs=[pl.BlockSpec(memory_space=any_)] * 14,
            out_specs=[pl.BlockSpec(memory_space=vm)] * 4,
            scratch_shapes=[
                vm((rows, width), BF16), vm((1, width), F32), vm((1, local_w), F32), vm((1, width), F32), vm((8, head_dim), F32),
                pltpu.SMEM((heads,), F32), vm((3, width, local_w), BF16), vm((width, local_w), BF16), vm((local_w, width), BF16),
                vm((width * reps, head_dim), BF16), vm((local_w, width), BF16),
                vm((2,) + state_shape, F32), vm((2,) + state_shape, F32), vm(state_shape, F32), vm(state_shape, F32),
                vm((rows, width), BF16), vm((128, head_dim), F32), vm((rows, local_w), F32), vm((rows, local_w), BF16),
                vm((128, 128 * reps), BF16), vm((16 * rows, head_dim), F32), vm((16 * rows, head_dim), F32),
                vm((8 * pairs, head_dim), F32), vm((8 * pairs, head_dim), F32), vm((4 * pairs, 8, head_dim), BF16),
                vm((4 * pairs, 8, shard_len), F32), vm((128, 128), F32), vm((4, 8, 128), F32), vm((128, 128), F32),
                vm((8 * pairs, head_dim), F32), vm((4 * pairs, 8, head_dim), F32), vm((4, pairs, 8, head_dim), F32),
                vm((rows, local_w), F32), vm((4, rows, 128), F32), vm((4, rows, width), F32), vm((4, rows, width), F32),
                vm((4, shard_len, head_dim), BF16),
                dma((NUM_SEMS,)), dma((NUM_SEMS,)), dma((17,)), dma((4,)),
            ],
            compiler_params=pltpu.CompilerParams(collective_id=0, has_side_effects=True, vmem_limit_bytes=46 * MIB),
        )(tokens, states, k_cache, v_cache, slopes, lin_gain.reshape(1, -1), w_qkv, w_lin_gate, out_gain.reshape(1, -1), w_lin_out, attn_gain.reshape(1, -1), w_in, w_attn_out, rope)
        bufs = [pltpu.with_memory_space_constraint(a, vm) for a in (k_buf, v_buf, s_buf, hid_buf)]
        return pl.pallas_call(
            write_kernel,
            name="write",
            out_shape=(jax.ShapeDtypeStruct((rows, width), BF16), jax.ShapeDtypeStruct(state_shape, F32),
                       jax.ShapeDtypeStruct(cache_shape, BF16), jax.ShapeDtypeStruct(cache_shape, BF16)),
            in_specs=[pl.BlockSpec(memory_space=vm)] * 4,
            out_specs=[pl.BlockSpec(memory_space=any_)] * 4,
            scratch_shapes=[dma((10,))],
            compiler_params=pltpu.CompilerParams(vmem_limit_bytes=20 * MIB),
        )(*bufs)

    batch_spec = P(('dp', 'sp'), None)
    head_spec = P(('dp', 'sp'), 'tp', None, None)
    cache_spec = P('dp', 'tp', 'sp', None)
    in_specs = (batch_spec, P('sp', 'dp', 'tp', None, None), cache_spec, cache_spec, P('tp'), P(None), P(None, None, 'tp'), P(None, 'tp'), P('tp'), P('tp', None), P(None), P(None, 'tp', None, None), P('tp', None))
    out_specs = (batch_spec, head_spec, head_spec, head_spec)
    return jax.shard_map(device_step, mesh=mesh, in_specs=in_specs, out_specs=out_specs, check_vma=False)
```

time: 347 us -> 213 us (0.61)
  the two profiles are of different devices: /device:TPU:0 before, /device:TPU:1 now
where the time goes in v1:
time: 213 us
  Pallas kernels  211 us (99%)
    pallas_call x1, Pallas kernels, device_step(): pl.pallas_call(step_kernel, name='step', out_shape=(vm(cache_shape, BF16)...  205 us
    pallas_call x1, Pallas kernels, device_step(): pl.pallas_call(write_kernel, name='write', out_shape=(jax.ShapeDtypeStruc...  6.15 us

profile of v1, /device:TPU:1, one launch (start us, length us, event | category | flops | bytes accessed | tf_op | source)
XLA Modules:
  0.0 213.1 jit_solution(5496213159303503359)
XLA Ops:
  0.6 1.3 reshape.21.out_gain
  1.9 205.1 %step.1 = (bf16[2,2,8208,128]{3,2,1,0:T(8,128)(2,1)S(1)}, bf16[2,2,8208,128]{3,2,1,0:T(8,128)(2,1)S(1)}, f32[2,6,128,128]{3,2,1,0:T(8,128)S(1)}, bf16[2,3072]{1,0:T(2,128)(2,1)S(1)}) custom-call(bf16[2,3072]{1,0:T(2,128)(2,1)} %tokens.1, f32[1,8,6,128,128]{4,3,2,1,0:T(8,128)} %states.1, bf16[8,2,2048,128]{3,2,1,0:T(8,128)(2,1)} %k_cache.1, ...), custom_call_target="tpu_custom_call" | custom-call | tf_op jit(solution)/shard_map/step/pallas_call | solution.py:406
  207.0 6.1 %write.1 = (bf16[2,3072]{1,0:T(2,128)(2,1)}, f32[2,6,128,128]{3,2,1,0:T(8,128)}, bf16[2,2,8208,128]{3,2,1,0:T(8,128)(2,1)}, bf16[2,2,8208,128]{3,2,1,0:T(8,128)(2,1)}) custom-call(bf16[2,2,8208,128]{3,2,1,0:T(8,128)(2,1)S(1)} %get-tuple-element.8.k_buf, bf16[2,2,8208,128]{3,2,1,0:T(8,128)(2,1)S(1)} %get-tuple-element.9.v_buf, ...), custom_call_target="tpu_custom_call" | custom-call | tf_op jit(solution)/shard_map/write/pallas_call | solution.py:429

commit v2 on v1

--- a/solution.py
+++ b/solution.py
@@ -25,6 +25,7 @@
 KV_NEAR = 21
 KV_FAR = 23
 NUM_SEMS = KV_FAR + 16
+LATE = 2
 
 
 def rope_table(head_dim, position):
@@ -55,9 +56,9 @@
     tokens, states, k_cache, v_cache, slopes, lin_gain, w_qkv, w_gate, out_gain, w_lin_out, attn_gain, w_in, w_attn_out, rope,
     k_buf, v_buf, s_out, hid,
     tok_v, lg_v, og_v, ag_v, rope_v, slope_s, qkv_v, gate_v, lout_v, in_v, aout_v,
-    st_loc, st_rcv, st_sum, st_in, hb, rows_v, o_v, g_v, rep_v, acc_v, proj_v, qf_v, vf_v, q_all, sc_v, mrow_v, m_all, mcol_v,
+    st_loc, st_rcv, st_sum, st_in, hb, rows_v, o_v, g_v, rep_v, acc_v, proj_v, qf_v, vf_v, qp_v, q_snd, q_all, sc_v, mrow_v, m_all, mcol_v,
     ns_v, ol_v, olr_v, ho_v, sq_all, po_all, pa_all, kst,
-    send, recv, lsem, ksem,
+    send, recv, lsem, ksem, met,
 ):
     sp = lax.axis_index("sp")
     tp = lax.axis_index("tp")
@@ -77,12 +78,31 @@
     def to_tp(off):
         return {"tp": lax.rem(tp + off, 4)}
 
+    core = lax.rem(sp, 2)
     barrier = pltpu.get_barrier_semaphore()
-    for i in (1, 2, 3):
+    for i in (2, 3, 1):
         pl.semaphore_signal(barrier, inc=1, device_id=to_sp(i), device_id_type=MESH)
-    for i in (1, 2, 3):
-        pl.semaphore_signal(barrier, inc=1, device_id=to_tp(i), device_id_type=MESH)
-    pl.semaphore_wait(barrier, 6)
+
+    @pl.when(core == 1)
+    def _():
+        pl.semaphore_wait(barrier, 3)
+        pl.semaphore_signal(met.at[0], inc=1, device_id=to_sp(1), device_id_type=MESH)
+
+    @pl.when(core == 0)
+    def _():
+        pl.semaphore_wait(met.at[0], 1)
+        for i in (1, 2, 3):
+            pl.semaphore_signal(barrier, inc=1, device_id=to_tp(i), device_id_type=MESH)
+
+    def meet_tp():
+        @pl.when(core == 0)
+        def _():
+            pl.semaphore_wait(barrier, 6)
+            pl.semaphore_signal(met.at[1], inc=1, device_id=to_sp(1), device_id_type=MESH)
+
+        @pl.when(core == 1)
+        def _():
+            pl.semaphore_wait(met.at[1], 1)
 
     def remote(src, dst, i, dev):
         return pltpu.make_async_remote_copy(src, dst, send.at[i], recv.at[i], device_id=dev, device_id_type=MESH)
@@ -91,17 +111,19 @@
         return pltpu.make_async_copy(src, dst, lsem.at[i])
 
     my_rows = pl.ds(pl.multiple_of(sp * shard_len, shard_len), shard_len)
+    pieces = [(t, b, j, mask) for t in range(2) for b in range(rows) for j in range(kv_dev) for mask in (2, 3)]
+    late = [(1, rows - 1, j, 2) for j in range(kv_dev)[-LATE:]]
+    pieces = [p for p in pieces if p not in late] + late
     far = []
-    for t, (src, dst) in enumerate(((k_cache, k_buf), (v_cache, v_buf))):
-        for b in range(rows):
-            for j in range(kv_dev):
-                for mask in (2, 3):
-                    far.append(remote(src.at[flip(sp, mask) * rows + b, j], dst.at[b, j, my_rows], KV_FAR + len(far), to_sp(mask)))
+    for t, b, j, mask in pieces:
+        src, dst = ((k_cache, k_buf), (v_cache, v_buf))[t]
+        far.append(remote(src.at[flip(sp, mask) * rows + b, j], dst.at[b, j, my_rows], KV_FAR + len(far), to_sp(mask)))
+    n_both = len(far) - len(late)
     far_state = [0, 0]
 
     def start_far(n):
         for _ in range(n):
-            if far_state[0] < len(far):
+            if far_state[0] < n_both:
                 far[far_state[0]].start()
                 far_state[0] += 1
 
@@ -209,13 +231,15 @@
             c.wait_send()
 
     sq_all[tp] = jnp.broadcast_to(jnp.sum(o * o, axis=-1, keepdims=True), (rows, 128))
+    meet_tp()
     cs = gather_tp(sq_all, SQ)
     pump(1)
     ld_og.wait()
     settle(cs)
     sq = ((sq_all[0] + sq_all[1]) + sq_all[2]) + sq_all[3]
     inv = lax.rsqrt(sq[:, :1] / (4 * local_w) + NORM_EPS)
-    g_v[...] = (o * inv * og_v[...] * gate).astype(BF16)
+    out_g = jnp.concatenate([og_v[h:h + 1, :] for h in range(heads)], axis=1)
+    g_v[...] = (o * inv * out_g * gate).astype(BF16)
 
     def project(x_ref, w_ref, dst):
         nb = 512
@@ -260,13 +284,16 @@
     proj_v[...] = proj
     acc_v[...] = (proj * rope_v[0:1] + partner * rope_v[1:2]).astype(BF16).astype(F32)
     qf_v[...] = jnp.zeros_like(qf_v)
+    qp_v[...] = jnp.zeros_like(qp_v)
     ns_v[...] = jnp.zeros_like(ns_v)
     tail_row = lax.broadcasted_iota(jnp.int32, (CACHE_EXTRA, head_dim), 0)
     for b in range(rows):
         for j in range(kv_dev):
             p = b * kv_dev + j
             for g in range(group):
-                qf_v[pl.ds(p * 8 + g, 1), :] = acc_v[pl.ds(b * 16 + g * kv_dev + j, 1), :]
+                q_row = acc_v[pl.ds(b * 16 + g * kv_dev + j, 1), :]
+                qf_v[pl.ds(p * 8 + g, 1), :] = q_row
+                qp_v[pl.ds(p * 4 + g, 1), :] = q_row
             k_new = acc_v[pl.ds(b * 16 + group * kv_dev + j, 1), :]
             v_new = proj_v[pl.ds(b * 16 + (group + 1) * kv_dev + j, 1), :]
             k_buf[b, j, pl.ds(prompt, CACHE_EXTRA), :] = jnp.where(tail_row == 0, k_new, 0.0).astype(BF16)
@@ -276,8 +303,8 @@
     qf = qf_v[...]
     pairs = rows * kv_dev
     my_pairs = pl.ds(sp * pairs, pairs)
-    q_all[my_pairs] = qf.astype(BF16).reshape(pairs, 8, head_dim)
-    cs = [remote(q_all.at[my_pairs], q_all.at[my_pairs], QX + i - 1, to_sp(i)) for i in (1, 2, 3)]
+    q_snd[sp] = qp_v[...].astype(BF16)
+    cs = [remote(q_snd.at[sp], q_snd.at[sp], QX + i - 1, to_sp(i)) for i in (1, 2, 3)]
     for c in cs:
         c.start()
     pump(2)
@@ -306,6 +333,10 @@
         fetch(k_cache, jnp.int32(i)).start()
     settle(cs)
     pump(1)
+    for d in range(4):
+        got = q_snd[d].astype(F32)
+        for p in range(pairs):
+            q_all[d * pairs + p] = jnp.concatenate([got[p * 4:p * 4 + 4], jnp.zeros((4, head_dim), F32)], axis=0).astype(BF16)
 
     def score_body(i, keys):
         s = lax.dot_general(q_all[i], keys, (((1,), (1,)), ((), ())), preferred_element_type=F32) * scale
@@ -317,22 +348,25 @@
         fetch(v_cache, jnp.int32(i)).start()
     my_m = pl.ds(pl.multiple_of(sp * pairs * 8, 8), pairs * 8)
     mrow_v[my_m, :] = jnp.maximum(mrow_v[my_m, :], ns_v[...])
-    m_all[sp] = jnp.transpose(mrow_v[...])[:8]
+    m_all[sp] = jnp.transpose(mrow_v[...])[:1]
     cs = [remote(m_all.at[sp], m_all.at[sp], MX + i - 1, to_sp(i)) for i in (1, 2, 3)]
     for c in cs:
         c.start()
     pump(1)
     settle(cs)
     m = jnp.maximum(jnp.maximum(m_all[0], m_all[1]), jnp.maximum(m_all[2], m_all[3]))
-    mcol_v[...] = jnp.transpose(jnp.broadcast_to(m[:1], (128, 128)))
+    mcol_v[...] = jnp.transpose(jnp.broadcast_to(m, (128, 128)))
     pump(1)
-    sub = lax.broadcasted_iota(jnp.int32, (8, head_dim), 0)
+    lane = lax.broadcasted_iota(jnp.int32, (1, head_dim), 1)
 
     def out_body(i, values):
         p = jnp.exp(sc_v[i] - mcol_v[pl.ds(pl.multiple_of(i * 8, 8), 8), :][:, :1])
-        total = jnp.broadcast_to(jnp.sum(p, axis=-1, keepdims=True), (8, head_dim))
+        total = jnp.sum(p, axis=-1, keepdims=True)
         o = jnp.dot(p.astype(BF16), values, preferred_element_type=F32)
-        ol_v[i] = jnp.where(sub < group, o, pltpu.roll(total, group, 0))
+        sums = jnp.zeros((1, head_dim), F32)
+        for g in range(group):
+            sums = jnp.where(lane == g, total[g:g + 1], sums)
+        ol_v[i] = jnp.concatenate([o[:group], sums], axis=0)
 
     stream(v_cache, 0, out_body)
     cs = [remote(ol_v.at[pl.ds(flip(sp, i) * pairs, pairs)], olr_v.at[sp], OX + i - 1, to_sp(i)) for i in (1, 2, 3)]
@@ -341,21 +375,27 @@
     olr_v[sp] = ol_v[my_pairs]
     pump(1)
     settle(cs)
-    total = (((olr_v[0] + olr_v[1]) + olr_v[2]) + olr_v[3]).reshape(pairs * 8, head_dim)
     new_p = jnp.exp(ns_v[...] - mcol_v[my_m, :])
-    denom = pltpu.roll(total, pairs * 8 - group, 0) + new_p
-    numer = total + new_p.astype(BF16).astype(F32) * vf_v[...]
-    qf_v[...] = numer / denom
+    new_o = new_p.astype(BF16).astype(F32) * vf_v[...]
     for b in range(rows):
         for j in range(kv_dev):
+            p = b * kv_dev + j
+            total = ((olr_v[0, p] + olr_v[1, p]) + olr_v[2, p]) + olr_v[3, p]
             for g in range(group):
-                h = j * group + g
-                ho_v[pl.ds(b, 1), h * head_dim:(h + 1) * head_dim] = qf_v[pl.ds((b * kv_dev + j) * 8 + g, 1), :]
+                h, at = j * group + g, p * 8 + g
+                denom = total[group:group + 1, g:g + 1] + new_p[at:at + 1]
+                ho_v[pl.ds(b, 1), h * head_dim:(h + 1) * head_dim] = (total[g:g + 1] + new_o[at:at + 1]) / denom
     g_v[...] = ho_v[...].astype(BF16)
     ld_aout.wait()
     project(g_v, aout_v, pa_all)
     cs = gather_tp(pa_all, PA)
     start_far(len(far))
+
+    @pl.when(core == 1)
+    def _():
+        for c in far[n_both:]:
+            c.start()
+
     settle(cs)
     att = ((pa_all[0] + pa_all[1]) + pa_all[2]) + pa_all[3]
     hid[...] = (RES_ALPHA * hb[...].astype(F32) + RES_BETA * att).astype(BF16)
@@ -367,13 +407,55 @@
         c.wait()
     for c in near:
         c.wait()
-    for c in far[far_state[1]:]:
+    for c in far[far_state[1]:n_both]:
         c.wait_send()
-    for c in far:
+    for c in far[:n_both]:
         c.wait_recv()
 
-
-def write_kernel(k_buf, v_buf, s_buf, hid_buf, hid, s_out, k_out, v_out, sem):
+    @pl.when(core == 1)
+    def _():
+        for c in far[n_both:]:
+            c.wait()
+
+
+def tail_kernel(v_cache, token, x_buf, send, recv):
+    sp = lax.axis_index("sp")
+    rows = v_cache.shape[0] // 4
+    kv_dev = v_cache.shape[1]
+    peer = flip(sp, 2)
+    barrier = pltpu.get_barrier_semaphore()
+    pl.semaphore_signal(barrier, inc=1, device_id={"sp": peer}, device_id_type=MESH)
+    pl.semaphore_wait(barrier, 1)
+
+    @pl.when(lax.rem(sp, 2) == 0)
+    def _():
+        cs = []
+        for i in range(LATE):
+            cs.append(pltpu.make_async_remote_copy(
+                v_cache.at[peer * rows + rows - 1, kv_dev - LATE + i], x_buf.at[i], send.at[i], recv.at[i], device_id={"sp": peer}, device_id_type=MESH))
+            cs[-1].start()
+        for c in cs:
+            c.wait()
+
+
+def tail_write_kernel(v_in, x_buf, v_out, sem):
+    sp = lax.axis_index("sp")
+    rows, kv_dev = v_out.shape[:2]
+    shard_len = x_buf.shape[1]
+
+    @pl.when(lax.rem(sp, 2) == 0)
+    def _():
+        cs = []
+        for i in range(LATE):
+            at = pl.ds(pl.multiple_of(flip(sp, 2) * shard_len, shard_len), shard_len)
+            cs.append(pltpu.make_async_copy(x_buf.at[i], v_out.at[rows - 1, kv_dev - LATE + i, at], sem.at[i]))
+            cs[-1].start()
+        for c in cs:
+            c.wait()
+
+
+def write_kernel(k_buf, v_buf, s_buf, hid_buf, hid, s_out, k_out, v_out, token, sem):
+    token[...] = jnp.zeros_like(token)
     cs = []
     for src, dst in ((k_buf, k_out), (v_buf, v_out)):
         for b in range(src.shape[0]):
@@ -396,6 +478,7 @@
         prompt = 4 * shard_len
         reps = w_attn_in.shape[1] * w_attn_in.shape[2]
         pairs = rows * kv_dev
+        group = heads // kv_dev
         cache_shape = (rows, kv_dev, prompt + CACHE_EXTRA, head_dim)
         state_shape = (rows, heads, head_dim, head_dim)
         vm, any_ = pltpu.VMEM, pl.ANY
@@ -410,32 +493,52 @@
             in_specs=[pl.BlockSpec(memory_space=any_)] * 14,
             out_specs=[pl.BlockSpec(memory_space=vm)] * 4,
             scratch_shapes=[
-                vm((rows, width), BF16), vm((1, width), F32), vm((1, local_w), F32), vm((1, width), F32), vm((8, head_dim), F32),
+                vm((rows, width), BF16), vm((1, width), F32), vm((heads, head_dim), F32), vm((1, width), F32), vm((8, head_dim), F32),
                 pltpu.SMEM((heads,), F32), vm((3, width, local_w), BF16), vm((width, local_w), BF16), vm((local_w, width), BF16),
                 vm((width * reps, head_dim), BF16), vm((local_w, width), BF16),
                 vm((2,) + state_shape, F32), vm((2,) + state_shape, F32), vm(state_shape, F32), vm(state_shape, F32),
                 vm((rows, width), BF16), vm((128, head_dim), F32), vm((rows, local_w), F32), vm((rows, local_w), BF16),
                 vm((128, 128 * reps), BF16), vm((16 * rows, head_dim), F32), vm((16 * rows, head_dim), F32),
-                vm((8 * pairs, head_dim), F32), vm((8 * pairs, head_dim), F32), vm((4 * pairs, 8, head_dim), BF16),
-                vm((4 * pairs, 8, shard_len), F32), vm((128, 128), F32), vm((4, 8, 128), F32), vm((128, 128), F32),
-                vm((8 * pairs, head_dim), F32), vm((4 * pairs, 8, head_dim), F32), vm((4, pairs, 8, head_dim), F32),
+                vm((8 * pairs, head_dim), F32), vm((8 * pairs, head_dim), F32), vm((4 * pairs, head_dim), F32), vm((4, 4 * pairs, head_dim), BF16), vm((4 * pairs, 8, head_dim), BF16),
+                vm((4 * pairs, 8, shard_len), F32), vm((128, 128), F32), vm((4, 1, 128), F32), vm((128, 128), F32),
+                vm((8 * pairs, head_dim), F32), vm((4 * pairs, group + 1, head_dim), F32), vm((4, pairs, group + 1, head_dim), F32),
                 vm((rows, local_w), F32), vm((4, rows, 128), F32), vm((4, rows, width), F32), vm((4, rows, width), F32),
                 vm((4, shard_len, head_dim), BF16),
-                dma((NUM_SEMS,)), dma((NUM_SEMS,)), dma((17,)), dma((4,)),
+                dma((NUM_SEMS,)), dma((NUM_SEMS,)), dma((17,)), dma((4,)), pltpu.SemaphoreType.REGULAR((2,)),
             ],
             compiler_params=pltpu.CompilerParams(collective_id=0, has_side_effects=True, vmem_limit_bytes=46 * MIB),
-        )(tokens, states, k_cache, v_cache, slopes, lin_gain.reshape(1, -1), w_qkv, w_lin_gate, out_gain.reshape(1, -1), w_lin_out, attn_gain.reshape(1, -1), w_in, w_attn_out, rope)
+        )(tokens, states, k_cache, v_cache, slopes, lin_gain.reshape(1, -1), w_qkv, w_lin_gate, out_gain.reshape(heads, head_dim), w_lin_out, attn_gain.reshape(1, -1), w_in, w_attn_out, rope)
         bufs = [pltpu.with_memory_space_constraint(a, vm) for a in (k_buf, v_buf, s_buf, hid_buf)]
-        return pl.pallas_call(
+        hid, s_out, k_out, v_out, token = pl.pallas_call(
             write_kernel,
             name="write",
             out_shape=(jax.ShapeDtypeStruct((rows, width), BF16), jax.ShapeDtypeStruct(state_shape, F32),
-                       jax.ShapeDtypeStruct(cache_shape, BF16), jax.ShapeDtypeStruct(cache_shape, BF16)),
+                       jax.ShapeDtypeStruct(cache_shape, BF16), jax.ShapeDtypeStruct(cache_shape, BF16), vm((8, 128), F32)),
             in_specs=[pl.BlockSpec(memory_space=vm)] * 4,
-            out_specs=[pl.BlockSpec(memory_space=any_)] * 4,
+            out_specs=[pl.BlockSpec(memory_space=any_)] * 4 + [pl.BlockSpec(memory_space=vm)],
             scratch_shapes=[dma((10,))],
             compiler_params=pltpu.CompilerParams(vmem_limit_bytes=20 * MIB),
         )(*bufs)
+        x_buf = pl.pallas_call(
+            tail_kernel,
+            name="tail",
+            out_shape=vm((LATE, shard_len, head_dim), BF16),
+            in_specs=[pl.BlockSpec(memory_space=any_), pl.BlockSpec(memory_space=vm)],
+            out_specs=pl.BlockSpec(memory_space=vm),
+            scratch_shapes=[dma((LATE,)), dma((LATE,))],
+            compiler_params=pltpu.CompilerParams(collective_id=1, has_side_effects=True, vmem_limit_bytes=4 * MIB),
+        )(pltpu.with_memory_space_constraint(v_cache, pltpu.HBM), pltpu.with_memory_space_constraint(token, vm))
+        v_out = pl.pallas_call(
+            tail_write_kernel,
+            name="tail_write",
+            out_shape=jax.ShapeDtypeStruct(cache_shape, BF16),
+            in_specs=[pl.BlockSpec(memory_space=any_), pl.BlockSpec(memory_space=vm)],
+            out_specs=pl.BlockSpec(memory_space=any_),
+            scratch_shapes=[dma((LATE,))],
+            input_output_aliases={0: 0},
+            compiler_params=pltpu.CompilerParams(vmem_limit_bytes=4 * MIB),
+        )(v_out, pltpu.with_memory_space_constraint(x_buf, vm))
+        return hid, s_out, k_out, v_out
 
     batch_spec = P(('dp', 'sp'), None)
     head_spec = P(('dp', 'sp'), 'tp', None, None)

time: 213 us -> 204 us (0.958); the launches traced: 213 us -> 200 us
  Pallas kernels: 211 us -> 200 us
    pallas_call x1, Pallas kernels: 205 us -> 192 us  [device_step(): pl.pallas_call(step_kernel, name='step', out_shape=(vm(cache_shape, BF16)...]
where the time goes in v2:
time: 204 us; the launch traced here: 200 us
  Pallas kernels  200 us (98%)
    pallas_call x1, Pallas kernels, device_step(): pl.pallas_call(step_kernel, name='step', out_shape=(vm(cache_shape, BF16)...  192 us
    pallas_call x1, Pallas kernels, device_step(): pl.pallas_call(write_kernel, name='write', out_shape=(jax.ShapeDtypeStruc...  6.15 us

profile of v2, /device:TPU:1, one launch (start us, length us, event | category | flops | bytes accessed | tf_op | source)
XLA Modules:
  0.0 200.5 jit_solution(17959767369077341661)
XLA Ops:
  0.6 191.7 %step.1 = (bf16[2,2,8208,128]{3,2,1,0:T(8,128)(2,1)S(1)}, bf16[2,2,8208,128]{3,2,1,0:T(8,128)(2,1)S(1)}, f32[2,6,128,128]{3,2,1,0:T(8,128)S(1)}, bf16[2,3072]{1,0:T(2,128)(2,1)S(1)}) custom-call(bf16[2,3072]{1,0:T(2,128)(2,1)} %tokens.1, f32[1,8,6,128,128]{4,3,2,1,0:T(8,128)} %states.1, bf16[8,2,2048,128]{3,2,1,0:T(8,128)(2,1)} %k_cache.1, ...), custom_call_target="tpu_custom_call" | custom-call | tf_op jit(solution)/shard_map/step/pallas_call | solution.py:489
  192.3 6.1 %write.1 = (bf16[2,3072]{1,0:T(2,128)(2,1)}, f32[2,6,128,128]{3,2,1,0:T(8,128)}, bf16[2,2,8208,128]{3,2,1,0:T(8,128)(2,1)}, bf16[2,2,8208,128]{3,2,1,0:T(8,128)(2,1)}, f32[8,128]{1,0:T(8,128)S(1)}) custom-call(bf16[2,2,8208,128]{3,2,1,0:T(8,128)(2,1)S(1)} %get-tuple-element.13.k_buf, bf16[2,2,8208,128]{3,2,1,0:T(8,128)(2,1)S(1)} %get-tuple-element.14.v_buf, ...), custom_call_target="tpu_custom_call" | custom-call | tf_op jit(solution)/shard_map/write/pallas_call | solution.py:512
  198.5 1.9 tail.1.x_buf
  (1 shorter events, 0.0 us)

commit v3 on v2

--- a/solution.py
+++ b/solution.py
@@ -83,24 +83,24 @@
     for i in (2, 3, 1):
         pl.semaphore_signal(barrier, inc=1, device_id=to_sp(i), device_id_type=MESH)
 
-    @pl.when(core == 1)
+    @pl.when(core == 0)
     def _():
         pl.semaphore_wait(barrier, 3)
         pl.semaphore_signal(met.at[0], inc=1, device_id=to_sp(1), device_id_type=MESH)
 
-    @pl.when(core == 0)
+    @pl.when(core == 1)
     def _():
         pl.semaphore_wait(met.at[0], 1)
         for i in (1, 2, 3):
             pl.semaphore_signal(barrier, inc=1, device_id=to_tp(i), device_id_type=MESH)
 
     def meet_tp():
-        @pl.when(core == 0)
+        @pl.when(core == 1)
         def _():
             pl.semaphore_wait(barrier, 6)
             pl.semaphore_signal(met.at[1], inc=1, device_id=to_sp(1), device_id_type=MESH)
 
-        @pl.when(core == 1)
+        @pl.when(core == 0)
         def _():
             pl.semaphore_wait(met.at[1], 1)
 
@@ -391,7 +391,7 @@
     cs = gather_tp(pa_all, PA)
     start_far(len(far))
 
-    @pl.when(core == 1)
+    @pl.when(core == 0)
     def _():
         for c in far[n_both:]:
             c.start()
@@ -412,7 +412,7 @@
     for c in far[:n_both]:
         c.wait_recv()
 
-    @pl.when(core == 1)
+    @pl.when(core == 0)
     def _():
         for c in far[n_both:]:
             c.wait()
@@ -427,7 +427,7 @@
     pl.semaphore_signal(barrier, inc=1, device_id={"sp": peer}, device_id_type=MESH)
     pl.semaphore_wait(barrier, 1)
 
-    @pl.when(lax.rem(sp, 2) == 0)
+    @pl.when(lax.rem(sp, 2) == 1)
     def _():
         cs = []
         for i in range(LATE):
@@ -443,7 +443,7 @@
     rows, kv_dev = v_out.shape[:2]
     shard_len = x_buf.shape[1]
 
-    @pl.when(lax.rem(sp, 2) == 0)
+    @pl.when(lax.rem(sp, 2) == 1)
     def _():
         cs = []
         for i in range(LATE):

time: 204 us -> 203 us (level); the launches traced: 200 us -> 203 us
    pallas_call x1, Pallas kernels: 1.95 us -> 15.3 us  [device_step(): pl.pallas_call(tail_kernel, name='tail', out_shape=vm((LATE, shard_len, h...]
    pallas_call x1, Pallas kernels: 192 us -> 180 us  [device_step(): pl.pallas_call(step_kernel, name='step', out_shape=(vm(cache_shape, BF16)...]
where the time goes in v3:
time: 203 us
  Pallas kernels  202 us (100%)
    pallas_call x1, Pallas kernels, device_step(): pl.pallas_call(step_kernel, name='step', out_shape=(vm(cache_shape, BF16)...  180 us
    pallas_call x1, Pallas kernels, device_step(): pl.pallas_call(tail_kernel, name='tail', out_shape=vm((LATE, shard_len, h...  15.3 us
    pallas_call x1, Pallas kernels, device_step(): pl.pallas_call(write_kernel, name='write', out_shape=(jax.ShapeDtypeStruc...  6.15 us

profile of v3, /device:TPU:1, one launch (start us, length us, event | category | flops | bytes accessed | tf_op | source)
XLA Modules:
  0.0 202.7 jit_solution(7181301248287414700)
XLA Ops:
  0.6 179.5 %step.1 = (bf16[2,2,8208,128]{3,2,1,0:T(8,128)(2,1)S(1)}, bf16[2,2,8208,128]{3,2,1,0:T(8,128)(2,1)S(1)}, f32[2,6,128,128]{3,2,1,0:T(8,128)S(1)}, bf16[2,3072]{1,0:T(2,128)(2,1)S(1)}) custom-call(bf16[2,3072]{1,0:T(2,128)(2,1)} %tokens.1, f32[1,8,6,128,128]{4,3,2,1,0:T(8,128)} %states.1, bf16[8,2,2048,128]{3,2,1,0:T(8,128)(2,1)} %k_cache.1, ...), custom_call_target="tpu_custom_call" | custom-call | tf_op jit(solution)/shard_map/step/pallas_call | solution.py:489
  180.1 6.1 %write.1 = (bf16[2,3072]{1,0:T(2,128)(2,1)}, f32[2,6,128,128]{3,2,1,0:T(8,128)}, bf16[2,2,8208,128]{3,2,1,0:T(8,128)(2,1)}, bf16[2,2,8208,128]{3,2,1,0:T(8,128)(2,1)}, f32[8,128]{1,0:T(8,128)S(1)}) custom-call(bf16[2,2,8208,128]{3,2,1,0:T(8,128)(2,1)S(1)} %get-tuple-element.13.k_buf, bf16[2,2,8208,128]{3,2,1,0:T(8,128)(2,1)S(1)} %get-tuple-element.14.v_buf, ...), custom_call_target="tpu_custom_call" | custom-call | tf_op jit(solution)/shard_map/write/pallas_call | solution.py:512
  186.3 15.3 %tail.1.x_buf = bf16[2,2048,128]{2,1,0:T(8,128)(2,1)S(1)} custom-call(bf16[8,2,2048,128]{3,2,1,0:T(8,128)(2,1)} %v_cache.3, f32[8,128]{1,0:T(8,128)S(1)} %get-tuple-element.21.token), custom_call_target="tpu_custom_call" | custom-call | tf_op jit(solution)/shard_map/tail/pallas_call | solution.py:522
  201.7 1.0 tail_write.1

commit v4 on v3

--- a/solution.py
+++ b/solution.py
@@ -57,7 +57,7 @@
     k_buf, v_buf, s_out, hid,
     tok_v, lg_v, og_v, ag_v, rope_v, slope_s, qkv_v, gate_v, lout_v, in_v, aout_v,
     st_loc, st_rcv, st_sum, st_in, hb, rows_v, o_v, g_v, rep_v, acc_v, proj_v, qf_v, vf_v, qp_v, q_snd, q_all, sc_v, mrow_v, m_all, mcol_v,
-    ns_v, ol_v, olr_v, ho_v, sq_all, po_all, pa_all, kst,
+    ns_v, ol_v, ol_sum, olr_v, ho_v, sq_all, po_all, pa_all, kst,
     send, recv, lsem, ksem, met,
 ):
     sp = lax.axis_index("sp")
@@ -80,29 +80,12 @@
 
     core = lax.rem(sp, 2)
     barrier = pltpu.get_barrier_semaphore()
-    for i in (2, 3, 1):
-        pl.semaphore_signal(barrier, inc=1, device_id=to_sp(i), device_id_type=MESH)
+    pl.semaphore_signal(barrier, inc=1, device_id=to_sp(2), device_id_type=MESH)
 
     @pl.when(core == 0)
     def _():
-        pl.semaphore_wait(barrier, 3)
-        pl.semaphore_signal(met.at[0], inc=1, device_id=to_sp(1), device_id_type=MESH)
-
-    @pl.when(core == 1)
-    def _():
-        pl.semaphore_wait(met.at[0], 1)
         for i in (1, 2, 3):
             pl.semaphore_signal(barrier, inc=1, device_id=to_tp(i), device_id_type=MESH)
-
-    def meet_tp():
-        @pl.when(core == 1)
-        def _():
-            pl.semaphore_wait(barrier, 6)
-            pl.semaphore_signal(met.at[1], inc=1, device_id=to_sp(1), device_id_type=MESH)
-
-        @pl.when(core == 0)
-        def _():
-            pl.semaphore_wait(met.at[1], 1)
 
     def remote(src, dst, i, dev):
         return pltpu.make_async_remote_copy(src, dst, send.at[i], recv.at[i], device_id=dev, device_id_type=MESH)
@@ -113,7 +96,8 @@
     my_rows = pl.ds(pl.multiple_of(sp * shard_len, shard_len), shard_len)
     pieces = [(t, b, j, mask) for t in range(2) for b in range(rows) for j in range(kv_dev) for mask in (2, 3)]
     late = [(1, rows - 1, j, 2) for j in range(kv_dev)[-LATE:]]
-    pieces = [p for p in pieces if p not in late] + late
+    pieces = sorted([p for p in pieces if p not in late], key=lambda p: p[0] > 0 or p[1] > 0) + late
+    pieces[1], pieces[2] = pieces[2], pieces[1]
     far = []
     for t, b, j, mask in pieces:
         src, dst = ((k_cache, k_buf), (v_cache, v_buf))[t]
@@ -133,13 +117,38 @@
             far_state[1] += 1
             start_far(1)
 
+    @pl.when(core == 1)
+    def _():
+        pl.semaphore_wait(barrier, 1)
+        far[0].start()
+        far[1].start()
+        pl.semaphore_signal(barrier, inc=1, device_id=to_sp(1), device_id_type=MESH)
+        pl.semaphore_wait(met.at[0], 1)
+
+    @pl.when(core == 0)
+    def _():
+        pl.semaphore_wait(barrier, 5)
+        pl.semaphore_signal(met.at[0], inc=1, device_id=to_sp(1), device_id_type=MESH)
+        far[0].start()
+        for i in (1, 2, 3):
+            pl.semaphore_signal(met.at[2], inc=1, device_id=to_tp(i), device_id_type=MESH)
+
+    def meet_tp():
+        @pl.when(core == 0)
+        def _():
+            pl.semaphore_wait(met.at[2], 3)
+            pl.semaphore_signal(met.at[1], inc=1, device_id=to_sp(1), device_id_type=MESH)
+
+        @pl.when(core == 1)
+        def _():
+            pl.semaphore_wait(met.at[1], 1)
+
     def st_rows(g):
         return pl.ds(g * rows, rows)
 
     st_own = remote(states.at[0, st_rows(flip(sp, 1))], st_rcv.at[0], ST_OWN, to_sp(1))
     st_fwd = remote(states.at[0, st_rows(flip(sp, 3))], st_rcv.at[1], ST_FWD, to_sp(1))
     st_fwd.start()
-    start_far(1)
     ld_fwd = local(states.at[0, st_rows(flip(sp, 2))], st_loc.at[1], 0)
     ld_slope = local(slopes, slope_s, 1)
     ld_fwd.start()
@@ -174,7 +183,13 @@
             st_sum[b, h] = w_me * st_loc[1, b, h] + w_ot * st_rcv[1, b, h]
     st_send = remote(st_sum, st_in, ST_SUM, to_sp(2))
     st_send.start()
-    start_far(2)
+
+    @pl.when(core == 0)
+    def _():
+        far[1].start()
+
+    far_state[0] = 2
+    start_far(1)
 
     ld_tok.wait()
     ld_lg.wait()
@@ -304,7 +319,7 @@
     pairs = rows * kv_dev
     my_pairs = pl.ds(sp * pairs, pairs)
     q_snd[sp] = qp_v[...].astype(BF16)
-    cs = [remote(q_snd.at[sp], q_snd.at[sp], QX + i - 1, to_sp(i)) for i in (1, 2, 3)]
+    cs = [remote(q_snd.at[sp], q_snd.at[sp], QX + i - 1, to_sp(i)) for i in (1, 2)]
     for c in cs:
         c.start()
     pump(2)
@@ -331,7 +346,13 @@
 
     for i in range(slots):
         fetch(k_cache, jnp.int32(i)).start()
-    settle(cs)
+    cs[1].wait_recv()
+    hand_on = remote(q_snd.at[flip(sp, 2)], q_snd.at[flip(sp, 2)], QX + 2, to_sp(1))
+    hand_on.start()
+    cs[0].wait_recv()
+    hand_on.wait_recv()
+    for c in cs + [hand_on]:
+        c.wait_send()
     pump(1)
     for d in range(4):
         got = q_snd[d].astype(F32)
@@ -369,18 +390,26 @@
         ol_v[i] = jnp.concatenate([o[:group], sums], axis=0)
 
     stream(v_cache, 0, out_body)
-    cs = [remote(ol_v.at[pl.ds(flip(sp, i) * pairs, pairs)], olr_v.at[sp], OX + i - 1, to_sp(i)) for i in (1, 2, 3)]
-    for c in cs:
-        c.start()
-    olr_v[sp] = ol_v[my_pairs]
+    o_fwd = remote(ol_v.at[pl.ds(flip(sp, 3) * pairs, pairs)], olr_v.at[1], OX, to_sp(1))
+    o_own = remote(ol_v.at[pl.ds(flip(sp, 1) * pairs, pairs)], olr_v.at[0], OX + 1, to_sp(1))
+    o_fwd.start()
+    o_own.start()
+    o_fwd.wait_recv()
+    ol_sum[...] = ol_v[pl.ds(flip(sp, 2) * pairs, pairs)] + olr_v[1]
+    o_sum = remote(ol_sum, olr_v.at[2], OX + 2, to_sp(2))
+    o_sum.start()
     pump(1)
-    settle(cs)
+    o_own.wait_recv()
+    o_sum.wait_recv()
+    for c in (o_fwd, o_own, o_sum):
+        c.wait_send()
+    mine = ol_v[my_pairs]
     new_p = jnp.exp(ns_v[...] - mcol_v[my_m, :])
     new_o = new_p.astype(BF16).astype(F32) * vf_v[...]
     for b in range(rows):
         for j in range(kv_dev):
             p = b * kv_dev + j
-            total = ((olr_v[0, p] + olr_v[1, p]) + olr_v[2, p]) + olr_v[3, p]
+            total = (mine[p] + olr_v[0, p]) + olr_v[2, p]
             for g in range(group):
                 h, at = j * group + g, p * 8 + g
                 denom = total[group:group + 1, g:g + 1] + new_p[at:at + 1]
@@ -501,10 +530,10 @@
                 vm((128, 128 * reps), BF16), vm((16 * rows, head_dim), F32), vm((16 * rows, head_dim), F32),
                 vm((8 * pairs, head_dim), F32), vm((8 * pairs, head_dim), F32), vm((4 * pairs, head_dim), F32), vm((4, 4 * pairs, head_dim), BF16), vm((4 * pairs, 8, head_dim), BF16),
                 vm((4 * pairs, 8, shard_len), F32), vm((128, 128), F32), vm((4, 1, 128), F32), vm((128, 128), F32),
-                vm((8 * pairs, head_dim), F32), vm((4 * pairs, group + 1, head_dim), F32), vm((4, pairs, group + 1, head_dim), F32),
+                vm((8 * pairs, head_dim), F32), vm((4 * pairs, group + 1, head_dim), F32), vm((pairs, group + 1, head_dim), F32), vm((3, pairs, group + 1, head_dim), F32),
                 vm((rows, local_w), F32), vm((4, rows, 128), F32), vm((4, rows, width), F32), vm((4, rows, width), F32),
                 vm((4, shard_len, head_dim), BF16),
-                dma((NUM_SEMS,)), dma((NUM_SEMS,)), dma((17,)), dma((4,)), pltpu.SemaphoreType.REGULAR((2,)),
+                dma((NUM_SEMS,)), dma((NUM_SEMS,)), dma((17,)), dma((4,)), pltpu.SemaphoreType.REGULAR((3,)),
             ],
             compiler_params=pltpu.CompilerParams(collective_id=0, has_side_effects=True, vmem_limit_bytes=46 * MIB),
         )(tokens, states, k_cache, v_cache, slopes, lin_gain.reshape(1, -1), w_qkv, w_lin_gate, out_gain.reshape(heads, head_dim), w_lin_out, attn_gain.reshape(1, -1), w_in, w_attn_out, rope)

time: 203 us -> 202 us (level)
  no operation moved by 1% of the time
where the time goes in v4:
time: 202 us
  Pallas kernels  201 us (100%)
    pallas_call x1, Pallas kernels, device_step(): pl.pallas_call(step_kernel, name='step', out_shape=(vm(cache_shape, BF16)...  178 us
    pallas_call x1, Pallas kernels, device_step(): pl.pallas_call(tail_kernel, name='tail', out_shape=vm((LATE, shard_len, h...  15.4 us
    pallas_call x1, Pallas kernels, device_step(): pl.pallas_call(write_kernel, name='write', out_shape=(jax.ShapeDtypeStruc...  6.15 us

profile of v4, /device:TPU:1, one launch (start us, length us, event | category | flops | bytes accessed | tf_op | source)
XLA Modules:
  0.0 201.7 jit_solution(9557874936265040670)
XLA Ops:
  0.6 178.5 %step.1 = (bf16[2,2,8208,128]{3,2,1,0:T(8,128)(2,1)S(1)}, bf16[2,2,8208,128]{3,2,1,0:T(8,128)(2,1)S(1)}, f32[2,6,128,128]{3,2,1,0:T(8,128)S(1)}, bf16[2,3072]{1,0:T(2,128)(2,1)S(1)}) custom-call(bf16[2,3072]{1,0:T(2,128)(2,1)} %tokens.1, f32[1,8,6,128,128]{4,3,2,1,0:T(8,128)} %states.1, bf16[8,2,2048,128]{3,2,1,0:T(8,128)(2,1)} %k_cache.1, ...), custom_call_target="tpu_custom_call" | custom-call | tf_op jit(solution)/shard_map/step/pallas_call | solution.py:518
  179.1 6.1 %write.1 = (bf16[2,3072]{1,0:T(2,128)(2,1)}, f32[2,6,128,128]{3,2,1,0:T(8,128)}, bf16[2,2,8208,128]{3,2,1,0:T(8,128)(2,1)}, bf16[2,2,8208,128]{3,2,1,0:T(8,128)(2,1)}, f32[8,128]{1,0:T(8,128)S(1)}) custom-call(bf16[2,2,8208,128]{3,2,1,0:T(8,128)(2,1)S(1)} %get-tuple-element.13.k_buf, bf16[2,2,8208,128]{3,2,1,0:T(8,128)(2,1)S(1)} %get-tuple-element.14.v_buf, ...), custom_call_target="tpu_custom_call" | custom-call | tf_op jit(solution)/shard_map/write/pallas_call | solution.py:541
  185.3 15.4 %tail.1.x_buf = bf16[2,2048,128]{2,1,0:T(8,128)(2,1)S(1)} custom-call(bf16[8,2,2048,128]{3,2,1,0:T(8,128)(2,1)} %v_cache.3, f32[8,128]{1,0:T(8,128)S(1)} %get-tuple-element.21.token), custom_call_target="tpu_custom_call" | custom-call | tf_op jit(solution)/shard_map/tail/pallas_call | solution.py:551
  200.7 1.0 tail_write.1

commit v5 on v4

--- a/solution.py
+++ b/solution.py
@@ -54,7 +54,7 @@
 
 def step_kernel(
     tokens, states, k_cache, v_cache, slopes, lin_gain, w_qkv, w_gate, out_gain, w_lin_out, attn_gain, w_in, w_attn_out, rope,
-    k_buf, v_buf, s_out, hid,
+    k_buf, v_buf, s_out, hid, x_src,
     tok_v, lg_v, og_v, ag_v, rope_v, slope_s, qkv_v, gate_v, lout_v, in_v, aout_v,
     st_loc, st_rcv, st_sum, st_in, hb, rows_v, o_v, g_v, rep_v, acc_v, proj_v, qf_v, vf_v, qp_v, q_snd, q_all, sc_v, mrow_v, m_all, mcol_v,
     ns_v, ol_v, ol_sum, olr_v, ho_v, sq_all, po_all, pa_all, kst,
@@ -167,16 +167,17 @@
     ld_aout = local(w_attn_out, aout_v, 14)
     own_kv = [local(src.at[st_rows(sp)], dst.at[:, :, my_rows], 15 + t) for t, (src, dst) in enumerate(((k_cache, k_buf), (v_cache, v_buf)))]
     near = [remote(src.at[st_rows(flip(sp, 1))], dst.at[:, :, my_rows], KV_NEAR + t, to_sp(1)) for t, (src, dst) in enumerate(((k_cache, k_buf), (v_cache, v_buf)))]
-    for c in [ld_own, ld_tok, ld_lg, ld_og, ld_ag, ld_rope] + ld_qkv + [ld_gate, ld_lout, ld_in, ld_aout] + near + own_kv:
+    ld_x = local(v_cache.at[flip(sp, 2) * rows + rows - 1, pl.ds(kv_dev - LATE, LATE)], x_src, 17)
+    for c in [ld_own, ld_tok, ld_lg, ld_og, ld_ag, ld_rope] + ld_qkv + [ld_gate, ld_lout, ld_in, ld_aout] + near + own_kv + [ld_x]:
         c.start()
 
     def decay(h, shard):
         off = (shard_len * (3 - shard)).astype(F32)
         return jnp.exp(jnp.full((1, head_dim), -slope_s[h] * off, F32))
 
+    st_fwd.wait_recv()
     ld_slope.wait()
     ld_fwd.wait()
-    st_fwd.wait_recv()
     for h in range(heads):
         w_me, w_ot = decay(h, sp), decay(h, flip(sp, 1))
         for b in range(rows):
@@ -191,6 +192,10 @@
     far_state[0] = 2
     start_far(1)
 
+    st_own.wait_recv()
+    st_send.wait_recv()
+    start_far(1)
+    ld_own.wait()
     ld_tok.wait()
     ld_lg.wait()
     x = tok_v[...].astype(F32)
@@ -217,9 +222,6 @@
             rows_v[pl.ds(16 + b * 8 + h, 1), :] = acts[1][b:b + 1, cols]
     cols_t = jnp.transpose(rows_v[...])
 
-    ld_own.wait()
-    st_own.wait_recv()
-    st_send.wait_recv()
     for h in range(heads):
         w_me, w_ot = decay(h, sp), decay(h, flip(sp, 1))
         lam = jnp.exp(jnp.full((1, head_dim), -slope_s[h], F32))
@@ -432,7 +434,7 @@
     st_own.wait_send()
     st_fwd.wait_send()
     st_send.wait_send()
-    for c in own_kv:
+    for c in own_kv + [ld_x]:
         c.wait()
     for c in near:
         c.wait()
@@ -447,10 +449,8 @@
             c.wait()
 
 
-def tail_kernel(v_cache, token, x_buf, send, recv):
+def tail_kernel(x_src, token, x_buf, send, recv):
     sp = lax.axis_index("sp")
-    rows = v_cache.shape[0] // 4
-    kv_dev = v_cache.shape[1]
     peer = flip(sp, 2)
     barrier = pltpu.get_barrier_semaphore()
     pl.semaphore_signal(barrier, inc=1, device_id={"sp": peer}, device_id_type=MESH)
@@ -461,7 +461,7 @@
         cs = []
         for i in range(LATE):
             cs.append(pltpu.make_async_remote_copy(
-                v_cache.at[peer * rows + rows - 1, kv_dev - LATE + i], x_buf.at[i], send.at[i], recv.at[i], device_id={"sp": peer}, device_id_type=MESH))
+                x_src.at[i], x_buf.at[i], send.at[i], recv.at[i], device_id={"sp": peer}, device_id_type=MESH))
             cs[-1].start()
         for c in cs:
             c.wait()
@@ -515,12 +515,13 @@
         w_in = jnp.transpose(w_attn_in, (0, 2, 1, 3)).reshape(width * reps, head_dim)
         rope = jnp.asarray(rope_table(head_dim, prompt))
         dma = pltpu.SemaphoreType.DMA
-        k_buf, v_buf, s_buf, hid_buf = pl.pallas_call(
+        x_shape = (LATE, shard_len, head_dim)
+        k_buf, v_buf, s_buf, hid_buf, x_src = pl.pallas_call(
             step_kernel,
             name="step",
-            out_shape=(vm(cache_shape, BF16), vm(cache_shape, BF16), vm(state_shape, F32), vm((rows, width), BF16)),
+            out_shape=(vm(cache_shape, BF16), vm(cache_shape, BF16), vm(state_shape, F32), vm((rows, width), BF16), vm(x_shape, BF16)),
             in_specs=[pl.BlockSpec(memory_space=any_)] * 14,
-            out_specs=[pl.BlockSpec(memory_space=vm)] * 4,
+            out_specs=[pl.BlockSpec(memory_space=vm)] * 5,
             scratch_shapes=[
                 vm((rows, width), BF16), vm((1, width), F32), vm((heads, head_dim), F32), vm((1, width), F32), vm((8, head_dim), F32),
                 pltpu.SMEM((heads,), F32), vm((3, width, local_w), BF16), vm((width, local_w), BF16), vm((local_w, width), BF16),
@@ -533,9 +534,9 @@
                 vm((8 * pairs, head_dim), F32), vm((4 * pairs, group + 1, head_dim), F32), vm((pairs, group + 1, head_dim), F32), vm((3, pairs, group + 1, head_dim), F32),
                 vm((rows, local_w), F32), vm((4, rows, 128), F32), vm((4, rows, width), F32), vm((4, rows, width), F32),
                 vm((4, shard_len, head_dim), BF16),
-                dma((NUM_SEMS,)), dma((NUM_SEMS,)), dma((17,)), dma((4,)), pltpu.SemaphoreType.REGULAR((3,)),
+                dma((NUM_SEMS,)), dma((NUM_SEMS,)), dma((18,)), dma((4,)), pltpu.SemaphoreType.REGULAR((3,)),
             ],
-            compiler_params=pltpu.CompilerParams(collective_id=0, has_side_effects=True, vmem_limit_bytes=46 * MIB),
+            compiler_params=pltpu.CompilerParams(collective_id=0, has_side_effects=True, vmem_limit_bytes=45 * MIB),
         )(tokens, states, k_cache, v_cache, slopes, lin_gain.reshape(1, -1), w_qkv, w_lin_gate, out_gain.reshape(heads, head_dim), w_lin_out, attn_gain.reshape(1, -1), w_in, w_attn_out, rope)
         bufs = [pltpu.with_memory_space_constraint(a, vm) for a in (k_buf, v_buf, s_buf, hid_buf)]
         hid, s_out, k_out, v_out, token = pl.pallas_call(
@@ -551,12 +552,12 @@
         x_buf = pl.pallas_call(
             tail_kernel,
             name="tail",
-            out_shape=vm((LATE, shard_len, head_dim), BF16),
-            in_specs=[pl.BlockSpec(memory_space=any_), pl.BlockSpec(memory_space=vm)],
+            out_shape=vm(x_shape, BF16),
+            in_specs=[pl.BlockSpec(memory_space=vm), pl.BlockSpec(memory_space=vm)],
             out_specs=pl.BlockSpec(memory_space=vm),
             scratch_shapes=[dma((LATE,)), dma((LATE,))],
             compiler_params=pltpu.CompilerParams(collective_id=1, has_side_effects=True, vmem_limit_bytes=4 * MIB),
-        )(pltpu.with_memory_space_constraint(v_cache, pltpu.HBM), pltpu.with_memory_space_constraint(token, vm))
+        )(pltpu.with_memory_space_constraint(x_src, vm), pltpu.with_memory_space_constraint(token, vm))
         v_out = pl.pallas_call(
             tail_write_kernel,
             name="tail_write",

time: 202 us -> 202 us (level)
  no operation moved by 1% of the time
where the time goes in v5:
time: 202 us
  Pallas kernels  201 us (100%)
    pallas_call x1, Pallas kernels, device_step(): pl.pallas_call(step_kernel, name='step', out_shape=(vm(cache_shape, BF16)...  178 us
    pallas_call x1, Pallas kernels, device_step(): pl.pallas_call(tail_kernel, name='tail', out_shape=vm(x_shape, BF16), in_...  15.4 us
    pallas_call x1, Pallas kernels, device_step(): pl.pallas_call(write_kernel, name='write', out_shape=(jax.ShapeDtypeStruc...  6.15 us

profile of v5, /device:TPU:1, one launch (start us, length us, event | category | flops | bytes accessed | tf_op | source)
XLA Modules:
  0.0 201.7 jit_solution(17249448916836667215)
XLA Ops:
  0.6 178.5 %step.1 = (bf16[2,2,8208,128]{3,2,1,0:T(8,128)(2,1)S(1)}, bf16[2,2,8208,128]{3,2,1,0:T(8,128)(2,1)S(1)}, f32[2,6,128,128]{3,2,1,0:T(8,128)S(1)}, bf16[2,3072]{1,0:T(2,128)(2,1)S(1)}, bf16[2,2048,128]{2,1,0:T(8,128)(2,1)S(1)}) custom-call(bf16[2,3072]{1,0:T(2,128)(2,1)} %tokens.1, f32[1,8,6,128,128]{4,3,2,1,0:T(8,128)} %states.1, ...), custom_call_target="tpu_custom_call" | custom-call | tf_op jit(solution)/shard_map/step/pallas_call | solution.py:519
  179.1 6.1 %write.1 = (bf16[2,3072]{1,0:T(2,128)(2,1)}, f32[2,6,128,128]{3,2,1,0:T(8,128)}, bf16[2,2,8208,128]{3,2,1,0:T(8,128)(2,1)}, bf16[2,2,8208,128]{3,2,1,0:T(8,128)(2,1)}, f32[8,128]{1,0:T(8,128)S(1)}) custom-call(bf16[2,2,8208,128]{3,2,1,0:T(8,128)(2,1)S(1)} %get-tuple-element.14.k_buf, bf16[2,2,8208,128]{3,2,1,0:T(8,128)(2,1)S(1)} %get-tuple-element.15.v_buf, ...), custom_call_target="tpu_custom_call" | custom-call | tf_op jit(solution)/shard_map/write/pallas_call | solution.py:542
  185.3 15.4 %tail.1.x_buf = bf16[2,2048,128]{2,1,0:T(8,128)(2,1)S(1)} custom-call(bf16[2,2048,128]{2,1,0:T(8,128)(2,1)S(1)} %get-tuple-element.22.x_src, f32[8,128]{1,0:T(8,128)S(1)} %get-tuple-element.23.token), custom_call_target="tpu_custom_call" | custom-call | tf_op jit(solution)/shard_map/tail/pallas_call | solution.py:552
  200.7 1.0 tail_write.1

commit v6 on v5

--- a/solution.py
+++ b/solution.py
@@ -400,7 +400,13 @@
     ol_sum[...] = ol_v[pl.ds(flip(sp, 2) * pairs, pairs)] + olr_v[1]
     o_sum = remote(ol_sum, olr_v.at[2], OX + 2, to_sp(2))
     o_sum.start()
-    pump(1)
+    start_far(len(far))
+
+    @pl.when(core == 0)
+    def _():
+        for c in far[n_both:]:
+            c.start()
+
     o_own.wait_recv()
     o_sum.wait_recv()
     for c in (o_fwd, o_own, o_sum):
@@ -420,13 +426,6 @@
     ld_aout.wait()
     project(g_v, aout_v, pa_all)
     cs = gather_tp(pa_all, PA)
-    start_far(len(far))
-
-    @pl.when(core == 0)
-    def _():
-        for c in far[n_both:]:
-            c.start()
-
     settle(cs)
     att = ((pa_all[0] + pa_all[1]) + pa_all[2]) + pa_all[3]
     hid[...] = (RES_ALPHA * hb[...].astype(F32) + RES_BETA * att).astype(BF16)

time: 202 us -> 202 us (level)
  no operation moved by 1% of the time
where the time goes in v6:
time: 202 us
  Pallas kernels  201 us (100%)
    pallas_call x1, Pallas kernels, device_step(): pl.pallas_call(step_kernel, name='step', out_shape=(vm(cache_shape, BF16)...  178 us
    pallas_call x1, Pallas kernels, device_step(): pl.pallas_call(tail_kernel, name='tail', out_shape=vm(x_shape, BF16), in_...  15.4 us
    pallas_call x1, Pallas kernels, device_step(): pl.pallas_call(write_kernel, name='write', out_shape=(jax.ShapeDtypeStruc...  6.15 us

profile of v6, /device:TPU:1, one launch (start us, length us, event | category | flops | bytes accessed | tf_op | source)
XLA Modules:
  0.0 201.7 jit_solution(18015554861605016826)
XLA Ops:
  0.6 178.5 %step.1 = (bf16[2,2,8208,128]{3,2,1,0:T(8,128)(2,1)S(1)}, bf16[2,2,8208,128]{3,2,1,0:T(8,128)(2,1)S(1)}, f32[2,6,128,128]{3,2,1,0:T(8,128)S(1)}, bf16[2,3072]{1,0:T(2,128)(2,1)S(1)}, bf16[2,2048,128]{2,1,0:T(8,128)(2,1)S(1)}) custom-call(bf16[2,3072]{1,0:T(2,128)(2,1)} %tokens.1, f32[1,8,6,128,128]{4,3,2,1,0:T(8,128)} %states.1, ...), custom_call_target="tpu_custom_call" | custom-call | tf_op jit(solution)/shard_map/step/pallas_call | solution.py:518
  179.1 6.1 %write.1 = (bf16[2,3072]{1,0:T(2,128)(2,1)}, f32[2,6,128,128]{3,2,1,0:T(8,128)}, bf16[2,2,8208,128]{3,2,1,0:T(8,128)(2,1)}, bf16[2,2,8208,128]{3,2,1,0:T(8,128)(2,1)}, f32[8,128]{1,0:T(8,128)S(1)}) custom-call(bf16[2,2,8208,128]{3,2,1,0:T(8,128)(2,1)S(1)} %get-tuple-element.14.k_buf, bf16[2,2,8208,128]{3,2,1,0:T(8,128)(2,1)S(1)} %get-tuple-element.15.v_buf, ...), custom_call_target="tpu_custom_call" | custom-call | tf_op jit(solution)/shard_map/write/pallas_call | solution.py:541
  185.3 15.4 %tail.1.x_buf = bf16[2,2048,128]{2,1,0:T(8,128)(2,1)S(1)} custom-call(bf16[2,2048,128]{2,1,0:T(8,128)(2,1)S(1)} %get-tuple-element.22.x_src, f32[8,128]{1,0:T(8,128)S(1)} %get-tuple-element.23.token), custom_call_target="tpu_custom_call" | custom-call | tf_op jit(solution)/shard_map/tail/pallas_call | solution.py:551
  200.7 1.0 tail_write.1

commit v7 on v6

--- a/solution.py
+++ b/solution.py
@@ -26,6 +26,7 @@
 KV_FAR = 23
 NUM_SEMS = KV_FAR + 16
 LATE = 2
+EARLY = 3
 
 
 def rope_table(head_dim, position):
@@ -103,6 +104,10 @@
         src, dst = ((k_cache, k_buf), (v_cache, v_buf))[t]
         far.append(remote(src.at[flip(sp, mask) * rows + b, j], dst.at[b, j, my_rows], KV_FAR + len(far), to_sp(mask)))
     n_both = len(far) - len(late)
+    cut = shard_len * EARLY // 16
+    head = remote(
+        v_cache.at[flip(sp, 2) * rows + rows - 1, pl.ds(kv_dev - LATE, LATE), pl.ds(0, cut)],
+        v_buf.at[rows - 1, pl.ds(kv_dev - LATE, LATE), pl.ds(pl.multiple_of(sp * shard_len, shard_len), cut)], KV_FAR + n_both, to_sp(2))
     far_state = [0, 0]
 
     def start_far(n):
@@ -167,7 +172,7 @@
     ld_aout = local(w_attn_out, aout_v, 14)
     own_kv = [local(src.at[st_rows(sp)], dst.at[:, :, my_rows], 15 + t) for t, (src, dst) in enumerate(((k_cache, k_buf), (v_cache, v_buf)))]
     near = [remote(src.at[st_rows(flip(sp, 1))], dst.at[:, :, my_rows], KV_NEAR + t, to_sp(1)) for t, (src, dst) in enumerate(((k_cache, k_buf), (v_cache, v_buf)))]
-    ld_x = local(v_cache.at[flip(sp, 2) * rows + rows - 1, pl.ds(kv_dev - LATE, LATE)], x_src, 17)
+    ld_x = local(v_cache.at[flip(sp, 2) * rows + rows - 1, pl.ds(kv_dev - LATE, LATE), pl.ds(cut, shard_len - cut)], x_src, 17)
     for c in [ld_own, ld_tok, ld_lg, ld_og, ld_ag, ld_rope] + ld_qkv + [ld_gate, ld_lout, ld_in, ld_aout] + near + own_kv + [ld_x]:
         c.start()
 
@@ -407,6 +412,10 @@
         for c in far[n_both:]:
             c.start()
 
+    @pl.when(core == 1)
+    def _():
+        head.start()
+
     o_own.wait_recv()
     o_sum.wait_recv()
     for c in (o_fwd, o_own, o_sum):
@@ -447,16 +456,20 @@
         for c in far[n_both:]:
             c.wait()
 
+    @pl.when(core == 1)
+    def _():
+        head.wait()
+
 
 def tail_kernel(x_src, token, x_buf, send, recv):
     sp = lax.axis_index("sp")
     peer = flip(sp, 2)
-    barrier = pltpu.get_barrier_semaphore()
-    pl.semaphore_signal(barrier, inc=1, device_id={"sp": peer}, device_id_type=MESH)
-    pl.semaphore_wait(barrier, 1)
 
     @pl.when(lax.rem(sp, 2) == 1)
     def _():
+        barrier = pltpu.get_barrier_semaphore()
+        pl.semaphore_signal(barrier, inc=1, device_id={"sp": peer}, device_id_type=MESH)
+        pl.semaphore_wait(barrier, 1)
         cs = []
         for i in range(LATE):
             cs.append(pltpu.make_async_remote_copy(
@@ -469,13 +482,14 @@
 def tail_write_kernel(v_in, x_buf, v_out, sem):
     sp = lax.axis_index("sp")
     rows, kv_dev = v_out.shape[:2]
-    shard_len = x_buf.shape[1]
+    shard_len = (v_out.shape[2] - CACHE_EXTRA) // 4
+    cut = shard_len - x_buf.shape[1]
 
     @pl.when(lax.rem(sp, 2) == 1)
     def _():
         cs = []
         for i in range(LATE):
-            at = pl.ds(pl.multiple_of(flip(sp, 2) * shard_len, shard_len), shard_len)
+            at = pl.ds(pl.multiple_of(flip(sp, 2) * shard_len + cut, 128), shard_len - cut)
             cs.append(pltpu.make_async_copy(x_buf.at[i], v_out.at[rows - 1, kv_dev - LATE + i, at], sem.at[i]))
             cs[-1].start()
         for c in cs:
@@ -514,7 +528,7 @@
         w_in = jnp.transpose(w_attn_in, (0, 2, 1, 3)).reshape(width * reps, head_dim)
         rope = jnp.asarray(rope_table(head_dim, prompt))
         dma = pltpu.SemaphoreType.DMA
-        x_shape = (LATE, shard_len, head_dim)
+        x_shape = (LATE, shard_len - shard_len * EARLY // 16, head_dim)
         k_buf, v_buf, s_buf, hid_buf, x_src = pl.pallas_call(
             step_kernel,
             name="step",

time: 202 us -> 202 us (level)
    pallas_call x1, Pallas kernels: 15.4 us -> 13.3 us  [device_step(): pl.pallas_call(tail_kernel, name='tail', out_shape=vm(x_shape, BF16), in_...]
    pallas_call x1, Pallas kernels: 178 us -> 181 us  [device_step(): pl.pallas_call(step_kernel, name='step', out_shape=(vm(cache_shape, BF16)...]
where the time goes in v7:
time: 202 us
  Pallas kernels  201 us (100%)
    pallas_call x1, Pallas kernels, device_step(): pl.pallas_call(step_kernel, name='step', out_shape=(vm(cache_shape, BF16)...  181 us
    pallas_call x1, Pallas kernels, device_step(): pl.pallas_call(tail_kernel, name='tail', out_shape=vm(x_shape, BF16), in_...  13.3 us
    pallas_call x1, Pallas kernels, device_step(): pl.pallas_call(write_kernel, name='write', out_shape=(jax.ShapeDtypeStruc...  6.15 us

profile of v7, /device:TPU:1, one launch (start us, length us, event | category | flops | bytes accessed | tf_op | source)
XLA Modules:
  0.0 201.6 jit_solution(14914976490794833996)
XLA Ops:
  0.6 180.6 %step.1 = (bf16[2,2,8208,128]{3,2,1,0:T(8,128)(2,1)S(1)}, bf16[2,2,8208,128]{3,2,1,0:T(8,128)(2,1)S(1)}, f32[2,6,128,128]{3,2,1,0:T(8,128)S(1)}, bf16[2,3072]{1,0:T(2,128)(2,1)S(1)}, bf16[2,1664,128]{2,1,0:T(8,128)(2,1)S(1)}) custom-call(bf16[2,3072]{1,0:T(2,128)(2,1)} %tokens.1, f32[1,8,6,128,128]{4,3,2,1,0:T(8,128)} %states.1, ...), custom_call_target="tpu_custom_call" | custom-call | tf_op jit(solution)/shard_map/step/pallas_call | solution.py:532
  181.2 6.1 %write.1 = (bf16[2,3072]{1,0:T(2,128)(2,1)}, f32[2,6,128,128]{3,2,1,0:T(8,128)}, bf16[2,2,8208,128]{3,2,1,0:T(8,128)(2,1)}, bf16[2,2,8208,128]{3,2,1,0:T(8,128)(2,1)}, f32[8,128]{1,0:T(8,128)S(1)}) custom-call(bf16[2,2,8208,128]{3,2,1,0:T(8,128)(2,1)S(1)} %get-tuple-element.14.k_buf, bf16[2,2,8208,128]{3,2,1,0:T(8,128)(2,1)S(1)} %get-tuple-element.15.v_buf, ...), custom_call_target="tpu_custom_call" | custom-call | tf_op jit(solution)/shard_map/write/pallas_call | solution.py:555
  187.4 13.3 %tail.1.x_buf = bf16[2,1664,128]{2,1,0:T(8,128)(2,1)S(1)} custom-call(bf16[2,1664,128]{2,1,0:T(8,128)(2,1)S(1)} %get-tuple-element.22.x_src, f32[8,128]{1,0:T(8,128)S(1)} %get-tuple-element.23.token), custom_call_target="tpu_custom_call" | custom-call | tf_op jit(solution)/shard_map/tail/pallas_call | solution.py:565
  200.7 0.9 tail_write.1

commit v8 on v7

--- a/solution.py
+++ b/solution.py
@@ -306,7 +306,6 @@
     proj_v[...] = proj
     acc_v[...] = (proj * rope_v[0:1] + partner * rope_v[1:2]).astype(BF16).astype(F32)
     qf_v[...] = jnp.zeros_like(qf_v)
-    qp_v[...] = jnp.zeros_like(qp_v)
     ns_v[...] = jnp.zeros_like(ns_v)
     tail_row = lax.broadcasted_iota(jnp.int32, (CACHE_EXTRA, head_dim), 0)
     for b in range(rows):
@@ -315,7 +314,7 @@
             for g in range(group):
                 q_row = acc_v[pl.ds(b * 16 + g * kv_dev + j, 1), :]
                 qf_v[pl.ds(p * 8 + g, 1), :] = q_row
-                qp_v[pl.ds(p * 4 + g, 1), :] = q_row
+                qp_v[pl.ds(p * group + g, 1), :] = q_row
             k_new = acc_v[pl.ds(b * 16 + group * kv_dev + j, 1), :]
             v_new = proj_v[pl.ds(b * 16 + (group + 1) * kv_dev + j, 1), :]
             k_buf[b, j, pl.ds(prompt, CACHE_EXTRA), :] = jnp.where(tail_row == 0, k_new, 0.0).astype(BF16)
@@ -364,7 +363,7 @@
     for d in range(4):
         got = q_snd[d].astype(F32)
         for p in range(pairs):
-            q_all[d * pairs + p] = jnp.concatenate([got[p * 4:p * 4 + 4], jnp.zeros((4, head_dim), F32)], axis=0).astype(BF16)
+            q_all[d * pairs + p] = jnp.concatenate([got[p * group:(p + 1) * group], jnp.zeros((8 - group, head_dim), F32)], axis=0).astype(BF16)
 
     def score_body(i, keys):
         s = lax.dot_general(q_all[i], keys, (((1,), (1,)), ((), ())), preferred_element_type=F32) * scale
@@ -470,13 +469,10 @@
         barrier = pltpu.get_barrier_semaphore()
         pl.semaphore_signal(barrier, inc=1, device_id={"sp": peer}, device_id_type=MESH)
         pl.semaphore_wait(barrier, 1)
-        cs = []
-        for i in range(LATE):
-            cs.append(pltpu.make_async_remote_copy(
-                x_src.at[i], x_buf.at[i], send.at[i], recv.at[i], device_id={"sp": peer}, device_id_type=MESH))
-            cs[-1].start()
-        for c in cs:
-            c.wait()
+        copy = pltpu.make_async_remote_copy(
+            x_src, x_buf, send.at[0], recv.at[0], device_id={"sp": peer}, device_id_type=MESH)
+        copy.start()
+        copy.wait()
 
 
 def tail_write_kernel(v_in, x_buf, v_out, sem):
@@ -487,13 +483,10 @@
 
     @pl.when(lax.rem(sp, 2) == 1)
     def _():
-        cs = []
-        for i in range(LATE):
-            at = pl.ds(pl.multiple_of(flip(sp, 2) * shard_len + cut, 128), shard_len - cut)
-            cs.append(pltpu.make_async_copy(x_buf.at[i], v_out.at[rows - 1, kv_dev - LATE + i, at], sem.at[i]))
-            cs[-1].start()
-        for c in cs:
-            c.wait()
+        at = pl.ds(pl.multiple_of(flip(sp, 2) * shard_len + cut, 128), shard_len - cut)
+        copy = pltpu.make_async_copy(x_buf, v_out.at[rows - 1, pl.ds(kv_dev - LATE, LATE), at], sem.at[0])
+        copy.start()
+        copy.wait()
 
 
 def write_kernel(k_buf, v_buf, s_buf, hid_buf, hid, s_out, k_out, v_out, token, sem):
@@ -542,7 +535,7 @@
                 vm((2,) + state_shape, F32), vm((2,) + state_shape, F32), vm(state_shape, F32), vm(state_shape, F32),
                 vm((rows, width), BF16), vm((128, head_dim), F32), vm((rows, local_w), F32), vm((rows, local_w), BF16),
                 vm((128, 128 * reps), BF16), vm((16 * rows, head_dim), F32), vm((16 * rows, head_dim), F32),
-                vm((8 * pairs, head_dim), F32), vm((8 * pairs, head_dim), F32), vm((4 * pairs, head_dim), F32), vm((4, 4 * pairs, head_dim), BF16), vm((4 * pairs, 8, head_dim), BF16),
+                vm((8 * pairs, head_dim), F32), vm((8 * pairs, head_dim), F32), vm((group * pairs, head_dim), F32), vm((4, group * pairs, head_dim), BF16), vm((4 * pairs, 8, head_dim), BF16),
                 vm((4 * pairs, 8, shard_len), F32), vm((128, 128), F32), vm((4, 1, 128), F32), vm((128, 128), F32),
                 vm((8 * pairs, head_dim), F32), vm((4 * pairs, group + 1, head_dim), F32), vm((pairs, group + 1, head_dim), F32), vm((3, pairs, group + 1, head_dim), F32),
                 vm((rows, local_w), F32), vm((4, rows, 128), F32), vm((4, rows, width), F32), vm((4, rows, width), F32),

time: 202 us -> 202 us (level)
  no operation moved by 1% of the time
where the time goes in v8:
time: 202 us
  Pallas kernels  201 us (100%)
    pallas_call x1, Pallas kernels, device_step(): pl.pallas_call(step_kernel, name='step', out_shape=(vm(cache_shape, BF16)...  181 us
    pallas_call x1, Pallas kernels, device_step(): pl.pallas_call(tail_kernel, name='tail', out_shape=vm(x_shape, BF16), in_...  13.3 us
    pallas_call x1, Pallas kernels, device_step(): pl.pallas_call(write_kernel, name='write', out_shape=(jax.ShapeDtypeStruc...  6.15 us

profile of v8, /device:TPU:1, one launch (start us, length us, event | category | flops | bytes accessed | tf_op | source)
XLA Modules:
  0.0 201.6 jit_solution(11691878387619443753)
XLA Ops:
  0.6 180.6 %step.1 = (bf16[2,2,8208,128]{3,2,1,0:T(8,128)(2,1)S(1)}, bf16[2,2,8208,128]{3,2,1,0:T(8,128)(2,1)S(1)}, f32[2,6,128,128]{3,2,1,0:T(8,128)S(1)}, bf16[2,3072]{1,0:T(2,128)(2,1)S(1)}, bf16[2,1664,128]{2,1,0:T(8,128)(2,1)S(1)}) custom-call(bf16[2,3072]{1,0:T(2,128)(2,1)} %tokens.1, f32[1,8,6,128,128]{4,3,2,1,0:T(8,128)} %states.1, ...), custom_call_target="tpu_custom_call" | custom-call | tf_op jit(solution)/shard_map/step/pallas_call | solution.py:525
  181.2 6.1 %write.1 = (bf16[2,3072]{1,0:T(2,128)(2,1)}, f32[2,6,128,128]{3,2,1,0:T(8,128)}, bf16[2,2,8208,128]{3,2,1,0:T(8,128)(2,1)}, bf16[2,2,8208,128]{3,2,1,0:T(8,128)(2,1)}, f32[8,128]{1,0:T(8,128)S(1)}) custom-call(bf16[2,2,8208,128]{3,2,1,0:T(8,128)(2,1)S(1)} %get-tuple-element.14.k_buf, bf16[2,2,8208,128]{3,2,1,0:T(8,128)(2,1)S(1)} %get-tuple-element.15.v_buf, ...), custom_call_target="tpu_custom_call" | custom-call | tf_op jit(solution)/shard_map/write/pallas_call | solution.py:548
  187.4 13.3 %tail.1.x_buf = bf16[2,1664,128]{2,1,0:T(8,128)(2,1)S(1)} custom-call(bf16[2,1664,128]{2,1,0:T(8,128)(2,1)S(1)} %get-tuple-element.22.x_src, f32[8,128]{1,0:T(8,128)S(1)} %get-tuple-element.23.token), custom_call_target="tpu_custom_call" | custom-call | tf_op jit(solution)/shard_map/tail/pallas_call | solution.py:558
  200.7 0.9 tail_write.1
